TPU v7x, 128 devices: a whole 4x4x4 slice. The times are simulated.
128 devices in a mesh: grp: 8 (over z, core), dev: 16 (over y, x).
Axes of the slice: x: 4, y: 4, z: 4, core: 2. Of those that a mesh axis runs over, the one named last changes fastest.
Arguments:
- points: float32 [3, 2097152], P(None, ('grp', 'dev')), may hold values from -6 to 6
- rhs: float32 [32, 2097152], P(None, ('grp', 'dev')), may hold values from -6 to 6
- leaf_count: int32 [8192], P(('grp', 'dev')), may hold values from 64 to 256
- near_list: int32 [8192, 8], P(('grp', 'dev')), may hold values from 0 to 8191, as said below
- leaf_basis: float32 [64, 2097152], P(None, ('grp', 'dev')), may hold values from -0.375 to 0.375
- leaf_transfer: float32 [64, 524288], P(None, ('grp', 'dev')), may hold values from -0.75 to 0.75
- leaf_parent: int32 [8192], P(('grp', 'dev')), may hold values from 0 to 1023, as said below
- nodes1: float32 [3, 65536], P(None, ('grp', 'dev')), may hold values from -6 to 6
- box_transfer: float32 [64, 65536], P(None, ('grp', 'dev')), may hold values from -0.75 to 0.75
- box_parent: int32 [1024], P(('grp', 'dev')), may hold values from 0 to 127, as said below
- far1: int32 [1024, 16], P(('grp', 'dev')), may hold values from 0 to 1023, as said below
- nodes2: float32 [3, 8192], replicated, may hold values from -6 to 6
- far2: int32 [128, 8], replicated, may hold values from 0 to 127, as said below
Outputs:
- result: float32 [32, 2097152], P(None, ('grp', 'dev'))
Inputs may be any that keep to these rules, and one draw needn't show every extreme that they name: `near_list`: row c begins with c itself; its other 7 entries are distinct leaf blocks of the same group of 1024 blocks (c // 1024 alike), each different from c by at most 32. `leaf_parent`: leaf c's box lies on the same device: it is one of boxes (c // 64) * 8 to (c // 64 + 1) * 8 - 1, and every box has exactly 8 leaves. `box_parent`: box b's parent belongs to its group: it is one of (b // 128) * 16 to (b // 128 + 1) * 16 - 1, and every level-2 box has exactly 8 children. `far1`: row t names 16 distinct level-1 boxes of t's group (b // 128 alike), never t. `far2`: row t names 8 distinct level-2 boxes, never t.
All inputs are finite; a program needn't handle non-finite values.
Results may differ from a plain program's by a relative error of at most 0.00011.
Values sent between devices are 32-bit elements; how exact they have to be, the bound alone decides.
A program may use at most 128 MiB of HBM per device.

v0:
```python
import functools

import jax
import jax.numpy as jnp
from jax import lax
from jax.experimental import pallas as pl
from jax.experimental.pallas import tpu as pltpu
from jax.sharding import PartitionSpec as P

B = 256
K = 64
R = 32
NEAR = 8
CHILD = 8
REACH = 32


HIGH = lax.Precision.HIGHEST


def edges(cells, axis, width):
    dim = cells.ndim - 1
    count = lax.axis_size(axis)
    head = lax.slice_in_dim(cells, 0, width, axis=dim)
    tail = lax.slice_in_dim(cells, cells.shape[dim] - width, cells.shape[dim], axis=dim)
    return (
        lax.ppermute(tail, axis, [(i, i + 1) for i in range(count - 1)]),
        lax.ppermute(head, axis, [(i + 1, i) for i in range(count - 1)]),
    )


def copy_for_each(x, axis):
    devices = lax.axis_size(axis)
    return lax.all_to_all(jnp.broadcast_to(x[None], (devices, *x.shape)), axis, 0, 0, tiled=True)


def laid_out(parts, dim):
    parts = jnp.moveaxis(parts, 0, dim)
    lengths = parts.shape
    return parts.reshape(*lengths[:dim], lengths[dim] * lengths[dim + 1], *lengths[dim + 2 :])


def gathered_copies(x, axis, dim):
    parts = copy_for_each(x, axis)
    return laid_out(parts, dim)


def gathered_total(x, axis):
    parts = lax.all_gather(x, axis)
    return parts.sum(axis=0)


def kernel(first, second):
    d_zero = first[0][:, None] - second[0][None, :]
    d_one = first[1][:, None] - second[1][None, :]
    d_two = first[2][:, None] - second[2][None, :]
    dist = d_zero * d_zero + d_one * d_one + d_two * d_two
    return lax.rsqrt(1.0 + 16.0 * dist)


def couple(target, sources, expansions):
    tiles = jax.vmap(lambda src: kernel(target, src))(sources)
    return jnp.einsum("sij,sjr->ir", tiles, expansions, precision=HIGH)


LANES = 128
TILE = 32
SLOTS = 2
NEAR_VMEM = 60 * 1024 * 1024


def near_kernel(leaves, cnt, rel, left_x, left_p, own_x, own_p, right_x, right_p, far, out, xs, pb, ab, lists, turns, accs):
    halo = left_x.shape[1] // B
    total = leaves + 2 * halo
    lane = lax.broadcasted_iota(jnp.int32, (R, B), 1)

    def fill(src_x, src_p, first, count):
        def one(i, carry):
            at = pl.ds(pl.multiple_of(i * B, B), B)
            to = pl.ds(pl.multiple_of((first + i) * B, B), B)
            x = jnp.where(lane < cnt[first + i], src_x[:, at], 0.0)
            high = x.astype(jnp.bfloat16)
            xs[0:R, to] = high
            xs[R : 2 * R, to] = (x - high.astype(jnp.float32)).astype(jnp.bfloat16)
            pb[0:3, to] = src_p[:, at] * 4.0
            return carry

        lax.fori_loop(0, count, one, 0, unroll=4)

    fill(left_x, left_p, 0, halo)
    fill(own_x, own_p, halo, leaves)
    fill(right_x, right_p, halo + leaves, halo)
    tail = pl.ds(total * B, 2 * LANES)
    xs[:, tail] = jnp.zeros((2 * R, 2 * LANES), jnp.bfloat16)
    pb[:, tail] = jnp.zeros((8, 2 * LANES), jnp.float32)

    def prepare(slot, target):
        place = slot * 24
        for n in range(NEAR):
            src = rel[target * NEAR + n]
            lists[place] = 2 * src
            lists[place + 1] = 2 * src + 1
            place = place + 1 + (cnt[src] > LANES).astype(jnp.int32)
        for n in range(3):
            lists[place + n] = 2 * total
        turns[slot] = (place - slot * 24 + 1) // 2
        for half in range(B // LANES):
            at = pl.ds(pl.multiple_of((halo + target) * B + half * LANES, LANES), LANES)
            flipped = pb[:, at].T
            for d in range(3):
                ab[slot, d, half * LANES : (half + 1) * LANES, :] = jnp.broadcast_to(
                    flipped[:, d : d + 1], (LANES, LANES)
                )

    def finish(slot, target):
        parts = []
        for half in range(B // LANES):
            rows = []
            for t in range(half * LANES // TILE, (half + 1) * LANES // TILE):
                rows.append(
                    pltpu.matmul_pop(accs[0][slot][t])[:, :LANES] + pltpu.matmul_pop(accs[1][slot][t])[:, :LANES]
                )
            flipped = jnp.concatenate(rows, axis=0).T
            parts.append(flipped[0:R] + flipped[R : 2 * R])
        at = pl.ds(pl.multiple_of(target * B, B), B)
        value = jnp.concatenate(parts, axis=1) + far[:, at]
        out[:, at] = jnp.where(lane < cnt[halo + target], value, 0.0)

    def couple_chunk(slot, tiles, units, first):
        blocks = []
        for unit in units:
            cols, weights = [], []
            for half in range(2):
                at = lists[first + 2 * unit + half]
                at = pl.ds(pl.multiple_of(at * LANES, LANES), LANES)
                weights.append(xs[:, at])
                cols.append([pb[d : d + 1, at] for d in range(3)])
            w = jnp.concatenate(weights, axis=1)
            pltpu.matmul_push_rhs(jnp.concatenate([w] * 4, axis=0), 0, unit, transpose=True)
            blocks.append(cols)
        for t in range(tiles):
            rows = pl.ds(t * TILE, TILE)
            own = [ab[slot, d, rows, :] for d in range(3)]
            for unit in units:
                highs, lows = [], []
                for half in range(2):
                    col = blocks[unit][half]
                    d0, d1, d2 = (own[d] - col[d] for d in range(3))
                    k = lax.rsqrt(((1.0 + d0 * d0) + d1 * d1) + d2 * d2)
                    high = k.astype(jnp.bfloat16)
                    highs.append(high)
                    lows.append((k - high.astype(jnp.float32)).astype(jnp.bfloat16))
                acc = accs[unit][slot][t]
                pltpu.matmul_acc_lhs(acc, jnp.concatenate(highs, axis=1), load_staged_rhs=0 if t == 0 else None)
                pltpu.matmul_acc_lhs(acc, jnp.concatenate(lows, axis=1))

    def sweep(slot, tiles):
        count = turns[slot]

        def pair(i, carry):
            couple_chunk(slot, tiles, (0, 1), slot * 24 + 4 * i)
            return carry

        lax.fori_loop(0, count // 2, pair, 0)

        @pl.when(count % 2 == 1)
        def _():
            couple_chunk(slot, tiles, (0,), slot * 24 + 2 * (count - 1))

    def group(g, carry):
        for slot in range(SLOTS):
            finish(slot, jnp.maximum(g - 1, 0) * SLOTS + slot)
            prepare(slot, jnp.minimum(g, leaves // SLOTS - 1) * SLOTS + slot)

        @pl.when(g < leaves // SLOTS)
        def _():
            for slot in range(SLOTS):
                kind = (cnt[halo + g * SLOTS + slot] + TILE - 1) // TILE - 2
                lax.switch(kind, [functools.partial(sweep, slot, tiles) for tiles in range(2, B // TILE + 1)])

        return carry

    lax.fori_loop(0, leaves // SLOTS + 1, group, 0)


def near_body(leaves, *refs):
    tiles = B // TILE
    specs = tuple(
        tuple(tuple(pltpu.ACC(unit)((TILE, 256), jnp.float32) for _ in range(tiles)) for _ in range(SLOTS))
        for unit in range(2)
    )
    pl.run_scoped(lambda accs: near_kernel(leaves, *refs, accs), specs)


def near_field(cnt, rel, left_x, left_p, own_x, own_p, right_x, right_p, far):
    leaves = own_x.shape[1] // B
    wide = (leaves + 2 * (left_x.shape[1] // B)) * B + 2 * LANES
    vmem = pl.BlockSpec(memory_space=pltpu.VMEM)
    smem = pl.BlockSpec(memory_space=pltpu.SMEM)
    return pl.pallas_call(
        functools.partial(near_body, leaves),
        out_shape=jax.ShapeDtypeStruct((R, leaves * B), jnp.float32),
        in_specs=[smem, smem] + [vmem] * 7,
        out_specs=vmem,
        scratch_shapes=[
            pltpu.VMEM((2 * R, wide), jnp.bfloat16),
            pltpu.VMEM((8, wide), jnp.float32),
            pltpu.VMEM((SLOTS, 3, B, LANES), jnp.float32),
            pltpu.SMEM((SLOTS * 24,), jnp.int32),
            pltpu.SMEM((SLOTS,), jnp.int32),
        ],
        compiler_params=pltpu.CompilerParams(vmem_limit_bytes=NEAR_VMEM),
        cost_estimate=pl.CostEstimate(flops=10**9, bytes_accessed=10**7, transcendentals=10**7),
        name="near_field",
    )(cnt, rel, left_x, left_p, own_x, own_p, right_x, right_p, far)


def local(
    points,
    rhs,
    leaf_count,
    near_list,
    leaf_basis,
    leaf_transfer,
    leaf_parent,
    nodes1,
    box_transfer,
    box_parent,
    far1,
    nodes2,
    far2,
):
    leaves = leaf_count.shape[0]
    n_dev = lax.axis_size("dev")
    group = lax.axis_index("grp")
    device = group * n_dev + lax.axis_index("dev")
    first_leaf = device * leaves
    slots = jnp.arange(B, dtype=jnp.int32)
    mask = (slots[None, :] < leaf_count[:, None]).astype(jnp.float32)
    masked = (rhs.reshape(R, leaves, B) * mask[None, :, :]).reshape(R, leaves * B)
    stacked = jnp.concatenate([points, masked], axis=0)
    width = REACH
    left, right = edges(stacked, "dev", width * B)
    left_count, right_count = edges(leaf_count, "dev", width)
    counts = jnp.concatenate([left_count, leaf_count, right_count])
    relative = (near_list - first_leaf + width).reshape(-1)
    basis = leaf_basis.reshape(K, leaves, B)
    values = masked.reshape(R, leaves, B)
    m_leaf = jnp.einsum("klb,rlb->lkr", basis, values, precision=HIGH)
    e_mats = leaf_transfer.reshape(K, leaves, K)
    lifted = jnp.einsum("ilj,lir->ljr", e_mats, m_leaf, precision=HIGH)
    local_boxes = nodes1.shape[1] // K
    leaf_owner = leaf_parent - device * local_boxes
    leaf_onehot = (leaf_owner[:, None] == jnp.arange(local_boxes, dtype=jnp.int32)[None, :]).astype(
        jnp.float32
    )
    m_one = jnp.einsum("lb,ljr->bjr", leaf_onehot, lifted, precision=HIGH)
    group_boxes = local_boxes * n_dev
    coarse_group = group_boxes // CHILD
    coarse_base = group * coarse_group
    local_parent = box_parent - coarse_base
    parent_onehot = (
        local_parent[:, None] == jnp.arange(coarse_group, dtype=jnp.int32)[None, :]
    ).astype(jnp.float32)
    f_mats = box_transfer.reshape(K, local_boxes, K)
    group_m, group_nodes = (gathered_copies(m_one, "dev", 0), gathered_copies(nodes1, "dev", 1))
    raised = jnp.einsum("ibj,bir->bjr", f_mats, m_one, precision=HIGH)
    part = jnp.einsum("bp,bjr->pjr", parent_onehot, raised, precision=HIGH)
    m_two_group = gathered_total(part, "dev")
    node_group = group_nodes.reshape(3, group_boxes, K).transpose(1, 0, 2)
    own_nodes = nodes1.reshape(3, local_boxes, K).transpose(1, 0, 2)
    far_local = far1 - group * group_boxes
    l_one = jax.vmap(lambda t, idx: couple(t, node_group[idx], group_m[idx]))(own_nodes, far_local)
    m_two = gathered_copies(m_two_group, "grp", 0)
    total_coarse = nodes2.shape[1] // K
    node_two = nodes2.reshape(3, total_coarse, K).transpose(1, 0, 2)
    far_group = lax.dynamic_slice_in_dim(far2, coarse_base, coarse_group, 0)
    target_nodes = lax.dynamic_slice_in_dim(node_two, coarse_base, coarse_group, 0)
    l_two = jax.vmap(lambda t, idx: couple(t, node_two[idx], m_two[idx]))(target_nodes, far_group)
    chosen = jnp.einsum("bp,pjr->bjr", parent_onehot, l_two, precision=HIGH)
    g_one = l_one + jnp.einsum("ibj,bjr->bir", f_mats, chosen, precision=HIGH)
    picked = jnp.einsum("lb,bjr->ljr", leaf_onehot, g_one, precision=HIGH)
    g_leaf = jnp.einsum("ilj,ljr->lir", e_mats, picked, precision=HIGH)
    far_part = jnp.einsum("klb,lkr->lrb", basis, g_leaf, precision=HIGH)
    far_part = far_part.transpose(1, 0, 2).reshape(R, leaves * B)
    return near_field(counts, relative, left[3:], left[:3], rhs, points, right[3:], right[:3], far_part)


def solution(mesh):
    placed = (
        P(None, ("grp", "dev")),
        P(None, ("grp", "dev")),
        P(("grp", "dev")),
        P(("grp", "dev"), None),
        P(None, ("grp", "dev")),
        P(None, ("grp", "dev")),
        P(("grp", "dev")),
        P(None, ("grp", "dev")),
        P(None, ("grp", "dev")),
        P(("grp", "dev")),
        P(("grp", "dev"), None),
        P(),
        P(),
    )
    return jax.shard_map(
        local, mesh=mesh, in_specs=placed, out_specs=P(None, ("grp", "dev")), check_vma=False
    )
```

profile of v0, /device:TPU:1, one launch (start us, length us, event | category | flops | bytes accessed | tf_op | source)
XLA Modules:
  0.0 265.4 jit_solution(14357815547058847841)
XLA Ops:
  6.6 2.1 reshape.70
  8.8 0.1 reshape.73
  8.9 6.9 %fusion.2 = f32[64,32,64]{2,1,0:T(8,128)S(1)} fusion(f32[8,64,8,256]{3,2,1,0:T(8,128)} %bitcast.89, f32[4,64,8,256]{3,2,1,0:T(8,128)} %bitcast.91, f32[64,256]{1,0:T(8,128)S(1)} %fusion.78), kind=kOutput, calls=%fused_computation.6 | convolution fusion | flops 403177472 | bytes 6881280 | tf_op jit(solution)/shard_map/klb,rlb->lkr/dot_general | solution.py:249
  15.9 3.1 %fusion.54 = f32[64,64,32]{1,2,0:T(8,128)S(1)} fusion(f32[64,32,64]{2,1,0:T(8,128)S(1)} %fusion.2, f32[64,64,64]{2,1,0:T(8,128)S(1)} %reshape.70), kind=kOutput, calls=%fused_computation.59 | convolution fusion | flops 100663296 | bytes 2097152 | tf_op jit(solution)/shard_map/ilj,lir->ljr/dot_general | solution.py:251
  19.0 1.0 fusion.66
  20.1 0.4 convolution_bitcast_fusion.1
  20.5 1.1 fusion.76
  21.6 0.7 broadcast_in_dim.10
  22.3 7.6 %all-to-all-start = ((f32[16,3,512]{2,1,0:T(4,128)}), f32[16,3,512]{2,1,0:T(4,128)S(1)}, u32[]{:S(2)}, u32[]{:S(2)}) async-start(f32[16,3,512]{2,1,0:T(4,128)} %broadcast_in_dim.10), calls=%async_computation | async-start | bytes 262144 | tf_op jit(solution)/shard_map/all_to_all | solution.py:34
  29.9 0.1 lt.42
  30.1 0.2 broadcast_multiply_fusion
  30.3 1.9 pad_maximum_fusion
  32.1 4.4 %collective-permute-start.2 = (f32[35,8192]{1,0:T(8,128)}, f32[35,8192]{1,0:T(8,128)}, u32[]{:S(2)}, u32[]{:S(2)}) collective-permute-start(f32[35,8192]{1,0:T(8,128)} %get-tuple-element.6), channel_id=1, source_target_pairs={{0,1},{1,2},{2,3},{3,4},{4,5},{5,6},{6,7},{7,8},{8,9},{9,10},{10,1... | collective-permute-start | bytes 3440648 | tf_op jit(solution)/shard_map/ppermute | solution.py:27
  36.6 1.3 collective-permute-start.3
  37.8 0.6 fusion.96
  38.4 4.5 %collective-permute-start = (s32[32]{0:T(128)}, s32[32]{0:T(128)}, u32[]{:S(2)}, u32[]{:S(2)}) collective-permute-start(s32[32]{0:T(128)} %get-tuple-element.19), channel_id=1, source_target_pairs={{0,1},{1,2},{2,3},{3,4},{4,5},{5,6},{6,7},{7,8},{8,9},{9,10},{10,1... | collective-permute-start | bytes 392 | tf_op jit(solution)/shard_map/ppermute | solution.py:27
  42.9 1.5 collective-permute-start.1
  44.7 0.6 reshape.94
  45.3 0.2 reshape.72
  45.5 0.3 broadcast_bitcast_fusion.1
  45.7 2.3 reshape.121
  48.1 7.6 %all-to-all-start.1 = ((f32[16,1,16384]{2,1,0:T(1,128)}), f32[16,1,16384]{2,1,0:T(1,128)S(1)}, u32[]{:S(2)}, u32[]{:S(2)}) async-start(f32[16,1,16384]{2,1,0:T(1,128)} %reshape.121), calls=%async_computation.1 | async-start | bytes 2097152 | tf_op jit(solution)/shard_map/all_to_all | solution.py:34
  55.7 0.6 pad_clamp_fusion
  56.3 1.1 copy.93
  57.4 0.1 reshape.67
  57.4 0.6 reshape.78
  58.1 0.8 gather_fusion.2
  58.8 0.6 slice_bitcast_fusion.5
  59.4 0.6 slice_bitcast_fusion.2
  60.0 0.8 fusion.94
  60.9 45.7 %all-gather.3.cloned.1.call-done = f32[256,64,32]{1,0,2:T(8,128)} async-done(((f32[16,64,32]{1,0,2:T(8,128)}), f32[256,64,32]{1,0,2:T(8,128)}) %all-gather.3.cloned.1.call-update) | async-done | bytes 2097168 | tf_op jit(solution)/shard_map/all_gather | solution.py:49
  106.5 2.6 reduce_sum.9
  109.1 0.1 copy.38
  109.2 0.3 broadcast_bitcast_fusion
  109.5 2.2 reshape.123
  111.6 6.7 %all-to-all-start.2 = ((f32[8,1,32768]{2,1,0:T(1,128)}), f32[8,1,32768]{2,1,0:T(1,128)}, u32[]{:S(2)}, u32[]{:S(2)}) async-start(f32[8,1,32768]{2,1,0:T(1,128)} %reshape.123), calls=%async_computation.2 | async-start | bytes 2097152 | tf_op jit(solution)/shard_map/all_to_all | solution.py:34
  118.4 0.7 pad_clamp_fusion.1
  119.0 0.1 copy.25
  119.1 0.7 reshape.66.refs_1_
  119.8 1.3 pad_add_fusion.refs_0_
  121.1 0.1 reshape_reshape.3
  121.2 0.1 copy.94
  121.4 0.8 gather_fusion
  122.1 0.8 fusion.95
  122.9 0.6 broadcast.52
  123.5 4.4 %reduce = f32[16,16384]{1,0:T(8,128)S(1)} reduce(f32[16,1,16384]{2,1,0:T(1,128)} %copy-done.4, f32[]{:T(128)} %broadcast.52), dimensions={1}, to_apply=%all_to_all.10.reduce_sub_computation | reduce | bytes 2097156 | tf_op jit(solution)/shard_map/all_to_all | solution.py:34
  128.0 0.8 reshape.122
  128.9 2.1 gather_fusion.1
  131.1 7.0 %fusion.62 = f32[8,64,32]{1,2,0:T(8,128)S(1)} fusion(f32[8,16,64,32]{2,3,1,0:T(8,128)} %bitcast.93, f32[8,16,64]{2,1,0:T(8,128)S(1)} %bitcast.108, f32[8,64]{1,0:T(8,128)S(1)} %copy-done.25, f32[8,16,64]{2,1,0:T(8,128)S(1)} %bitcast.107, f32[8,64]{1,0:T(8,128)S(1)} %copy-done.26, f32[8,16,64]{2,1,0:T(8,128)S(1)} %bitcast.106, f32[8,64]{1,0:T(8,128)S(1)} %copy-done.24), kind=kOutput, calls=%fused_computation.66 | convolution fusion | flops 206569472 | bytes 1218560 | tf_op jit(solution)/shard_map/vmap(sij,sjr->ir)/dot_general | solution.py:63
  138.1 2.5 slice.90.refs_2_
  140.6 1.6 slice.91.refs_3_
  142.2 2.4 slice.92.refs_6_
  144.6 1.6 slice.93.refs_7_
  146.2 13.9 %reduce.1 = f32[8,32768]{1,0:T(8,128)S(1)} reduce(f32[8,1,32768]{2,1,0:T(1,128)} %all-to-all-done.2, f32[]{:T(128)} %broadcast.52), dimensions={1}, to_apply=%all_to_all.11.reduce_sub_computation | reduce | bytes 2097156 | tf_op jit(solution)/shard_map/all_to_all | solution.py:34
  160.1 0.8 reshape.124
  161.0 2.1 gather_fusion.3
  163.3 6.9 %fusion.58 = f32[16,64,32]{1,2,0:T(8,128)S(1)} fusion(f32[16,8,64,32]{2,3,1,0:T(8,128)} %bitcast.92, f32[16,8,64]{2,1,0:T(8,128)S(1)} %bitcast.105, f32[16,64]{1,0:T(8,128)S(1)} %copy-done.19, f32[16,8,64]{2,1,0:T(8,128)S(1)} %bitcast.104, f32[16,64]{1,0:T(8,128)S(1)} %copy-done.20, f32[16,8,64]{2,1,0:T(8,128)S(1)} %bitcast.103, f32[16,64]{1,0:T(8,128)S(1)} %copy-done.18), kind=kOutput, calls=%fused_computation.62 | convolution fusion | flops 206569472 | bytes 1290240 | tf_op jit(solution)/shard_map/vmap(sij,sjr->ir)/dot_general | solution.py:63
  170.2 0.4 fusion.69
  170.6 0.6 fusion.61
  171.1 0.6 fusion.73
  171.8 5.0 %fusion.47 = f32[64,32,64]{2,1,0:T(8,128)S(1)} fusion(f32[64,64,64]{2,1,0:T(8,128)S(1)} %copy-done.1, f32[64,64,32]{1,0,2:T(8,128)S(1)} %fusion.73), kind=kOutput, calls=%fused_computation.54 | convolution fusion | flops 100663296 | bytes 2097152 | tf_op jit(solution)/shard_map/ilj,ljr->lir/dot_general | solution.py:283
  176.8 2.4 fusion.51
  179.2 1.5 copy.51
  180.7 77.6 %near_field.1 = f32[32,16384]{1,0:T(8,128)} custom-call(s32[128]{0:T(128)} %pad_add_fusion.refs_0_, s32[512]{0:T(512)} %reshape.66.refs_1_, f32[32,8192]{1,0:T(8,128)} %slice.90.refs_2_, f32[3,8192]{1,0:T(4,128)} %slice.91.refs_3_, f32[32,16384]{1,0:T(8,128)} %refs_4_.1, f32[3,16384]{1,0:T(4,128)} %refs_5_.1, f32[32,8192]{1,0:T(8,128)} %slice.92.refs_6_, ...), custom_call_target="tpu_custom_call" | custom-call | flops 1000000000 | bytes 10000000 | tf_op jit(solution)/shard_map/near_field/pallas_call | solution.py:200
  (88 shorter events, 0.6 us)
Async XLA Ops:
  6.5 2.1 copy-start.16
  6.5 2.2 copy-start.7
  6.5 2.3 copy-start.31
  6.5 2.4 copy-start.32
  6.5 100.0 %all-gather.3.cloned.1.call-start = ((), (), s32[]{:S(2)}) async-start(), calls=%async_computation.3 | async-start | bytes 4456448 | tf_op jit(solution)/shard_map/all_gather | solution.py:49
  8.7 7.2 %copy-start = (f32[64,64,64]{2,1,0:T(8,128)}, f32[64,64,64]{2,1,0:T(8,128)S(1)}, u32[]{:S(2)}) copy-start(f32[64,64,64]{2,1,0:T(8,128)S(1)} %reshape.70) | copy-start | bytes 3145732
  8.9 11.6 %copy-start.29 = (s32[8]{0:T(128)}, s32[8]{0:T(128)S(1)}, u32[]{:S(2)}) copy-start(s32[8]{0:T(128)S(1)} %broadcast_subtract_fusion) | copy-start | bytes 100
  8.9 10.1 %copy-start.27 = (s32[64]{0:T(128)}, s32[64]{0:T(128)S(1)}, u32[]{:S(2)}) copy-start(s32[64]{0:T(128)S(1)} %broadcast_subtract_fusion.1) | copy-start | bytes 772
  15.9 5.7 %copy-start.15 = (f32[3,512]{1,0:T(4,128)S(1)}, f32[3,512]{1,0:T(4,128)}, u32[]{:S(2)}) copy-start(f32[3,512]{1,0:T(4,128)} %param.20) | copy-start | bytes 18436
  19.0 11.1 %copy-start.3 = (f32[32,16384]{1,0:T(8,128)S(1)}, f32[32,16384]{1,0:T(8,128)}, u32[]{:S(2)}) copy-start(f32[32,16384]{1,0:T(8,128)} %refs_4_.1) | copy-start | bytes 6291460
  21.6 8.6 %copy-start.6 = (f32[3,16384]{1,0:T(4,128)S(1)}, f32[3,16384]{1,0:T(4,128)}, u32[]{:S(2)}) copy-start(f32[3,16384]{1,0:T(4,128)} %refs_5_.1) | copy-start | bytes 589828
  22.3 25.8 %all-to-all-start = ((f32[16,3,512]{2,1,0:T(4,128)}), f32[16,3,512]{2,1,0:T(4,128)S(1)}, u32[]{:S(2)}, u32[]{:S(2)}) async-start(f32[16,3,512]{2,1,0:T(4,128)} %broadcast_in_dim.10), calls=%async_computation | async-start | bytes 262144 | tf_op jit(solution)/shard_map/all_to_all | solution.py:34
  30.2 14.3 %copy-start.21 = (s32[128,8]{0,1:T(8,128)S(1)}, s32[128,8]{0,1:T(8,128)}, u32[]{:S(2)}) copy-start(s32[128,8]{0,1:T(8,128)} %param.25) | copy-start | bytes 12292
  30.3 15.1 %copy-start.8 = (f32[3,8192]{1,0:T(4,128)S(1)}, f32[3,8192]{1,0:T(4,128)}, u32[]{:S(2)}) copy-start(f32[3,8192]{1,0:T(4,128)} %param.24) | copy-start | bytes 294916
  32.1 106.0 %collective-permute-start.2 = (f32[35,8192]{1,0:T(8,128)}, f32[35,8192]{1,0:T(8,128)}, u32[]{:S(2)}, u32[]{:S(2)}) collective-permute-start(f32[35,8192]{1,0:T(8,128)} %get-tuple-element.6), channel_id=1, source_target_pairs={{0,1},{1,2},{2,3},{3,4},{4,5},{5,6},{6,7},{7,8},{8,9},{9,10},{10,1... | collective-permute-start | bytes 3440648 | tf_op jit(solution)/shard_map/ppermute | solution.py:27
  36.6 105.7 %collective-permute-start.3 = (f32[35,8192]{1,0:T(8,128)}, f32[35,8192]{1,0:T(8,128)}, u32[]{:S(2)}, u32[]{:S(2)}) collective-permute-start(f32[35,8192]{1,0:T(8,128)} %get-tuple-element.5), channel_id=1, source_target_pairs={{1,0},{2,1},{3,2},{4,3},{5,4},{6,5},{7,6},{8,7},{9,8},{10,9},{11,1... | collective-permute-start | bytes 3440648 | tf_op jit(solution)/shard_map/ppermute | solution.py:28
  38.4 81.4 %collective-permute-start = (s32[32]{0:T(128)}, s32[32]{0:T(128)}, u32[]{:S(2)}, u32[]{:S(2)}) collective-permute-start(s32[32]{0:T(128)} %get-tuple-element.19), channel_id=1, source_target_pairs={{0,1},{1,2},{2,3},{3,4},{4,5},{5,6},{6,7},{7,8},{8,9},{9,10},{10,1... | collective-permute-start | bytes 392 | tf_op jit(solution)/shard_map/ppermute | solution.py:27
  42.9 76.9 %collective-permute-start.1 = (s32[32]{0:T(128)}, s32[32]{0:T(128)}, u32[]{:S(2)}, u32[]{:S(2)}) collective-permute-start(s32[32]{0:T(128)} %get-tuple-element.20), channel_id=1, source_target_pairs={{1,0},{2,1},{3,2},{4,3},{5,4},{6,5},{7,6},{8,7},{9,8},{10,9},{11,1... | collective-permute-start | bytes 392 | tf_op jit(solution)/shard_map/ppermute | solution.py:28
  45.5 2.6 copy-start.5
  45.5 2.6 copy-start.22
  45.5 2.6 copy-start.23
  48.1 63.5 %all-to-all-start.1 = ((f32[16,1,16384]{2,1,0:T(1,128)}), f32[16,1,16384]{2,1,0:T(1,128)S(1)}, u32[]{:S(2)}, u32[]{:S(2)}) async-start(f32[16,1,16384]{2,1,0:T(1,128)} %reshape.121), calls=%async_computation.1 | async-start | bytes 2097152 | tf_op jit(solution)/shard_map/all_to_all | solution.py:34
  109.5 10.4 %copy-start.17 = (s32[64]{0:T(128)S(1)}, s32[64]{0:T(128)}, u32[]{:S(2)}) copy-start(s32[64]{0:T(128)} %param.15) | copy-start | bytes 772
  111.6 11.3 %copy-start.4 = (f32[16,1,16384]{2,1,0:T(1,128)}, f32[16,1,16384]{2,1,0:T(1,128)S(1)}, u32[]{:S(2)}) copy-start(f32[16,1,16384]{2,1,0:T(1,128)S(1)} %all-to-all-done.1) | copy-start | bytes 3145732
  111.6 34.6 %all-to-all-start.2 = ((f32[8,1,32768]{2,1,0:T(1,128)}), f32[8,1,32768]{2,1,0:T(1,128)}, u32[]{:S(2)}, u32[]{:S(2)}) async-start(f32[8,1,32768]{2,1,0:T(1,128)} %reshape.123), calls=%async_computation.2 | async-start | bytes 2097152 | tf_op jit(solution)/shard_map/all_to_all | solution.py:34
  128.8 2.2 copy-start.12
  128.8 2.2 copy-start.13
  128.8 2.2 copy-start.14
  128.9 2.2 copy-start.24
  128.9 2.2 copy-start.25
  128.9 2.2 copy-start.26
  161.0 2.2 copy-start.9
  161.0 2.2 copy-start.10
  161.0 2.2 copy-start.11
  161.0 2.2 copy-start.18
  161.0 2.2 copy-start.19
  161.0 2.2 copy-start.20
  163.2 6.9 %copy-start.30 = (s32[8]{0:T(128)S(1)}, s32[8]{0:T(128)}, u32[]{:S(2)}) copy-start(s32[8]{0:T(128)} %copy-done.29) | copy-start | bytes 100
  163.2 7.9 %copy-start.28 = (s32[64]{0:T(128)S(1)}, s32[64]{0:T(128)}, u32[]{:S(2)}) copy-start(s32[64]{0:T(128)} %copy-done.27) | copy-start | bytes 772
  170.2 1.6 copy-start.1
  171.1 5.7 %copy-start.2 = (f32[64,16384]{1,0:T(8,128)S(1)}, f32[64,16384]{1,0:T(8,128)}, u32[]{:S(2)}) copy-start(f32[64,16384]{1,0:T(8,128)} %param.17) | copy-start | bytes 12582916
Sparse Core Ops, SparseCore 0:
  21.7 84.7 all-gather.2
where the time goes:
time: 269 us; the launch traced here: 265 us
  Pallas kernels  77.6 us (29%)
  waiting for transfers between devices  45.7 us (17%)
  matrix products  35.4 us (13%)
  starting transfers between devices  33.6 us (12%)
  local copies, waits for them, and re-layouts  33 us (12%)
  other arithmetic  25.7 us (10%)
  between operations  14.3 us (5%)
    pallas_call x1, Pallas kernels, near_field(): pl.pallas_call(functools.partial(near_body, leaves), out_shape=jax.ShapeD...  77.6 us
    all_gather x1, waiting for transfers between devices, gathered_total(): parts = lax.all_gather(x, axis)  45.7 us
    all_to_all x3, starting transfers between devices, copy_for_each(): lax.all_to_all(jnp.broadcast_to(x[None], (devices, *x.shape)), axis, 0, 0...  21.9 us
    all_to_all x2, other arithmetic, copy_for_each(): lax.all_to_all(jnp.broadcast_to(x[None], (devices, *x.shape)), axis, 0, 0...  18.4 us
    dot_general x2, matrix products, couple(): return jnp.einsum('sij,sjr->ir', tiles, expansions, precision=HIGH)  13.9 us
    ppermute x2, starting transfers between devices, edges(): lax.ppermute(tail, axis, [(i, i + 1) for i in range(count - 1)])  8.91 us
    dot_general x1, matrix products, local(): m_leaf = jnp.einsum('klb,rlb->lkr', basis, values, precision=HIGH)  6.92 us
    unnamed x74, local copies, waits for them, and re-layouts  6.81 us
  transfers between devices with their start and end apart: 8, of which 1 were waited for; matrix products, arithmetic and copies ran while one was open for 17% of the time, Pallas kernels for 0%

commit v1 on v0

v1 whole, which is shorter than its diff:
```python
import functools

import jax
import jax.numpy as jnp
from jax import lax
from jax.experimental import pallas as pl
from jax.experimental.pallas import tpu as pltpu
from jax.sharding import PartitionSpec as P

B = 256
K = 64
R = 32
NEAR = 8
REACH = 32
LANES = 128
TILE = 32
SLOTS = 2
NEAR_VMEM = 60 * 1024 * 1024


def near_kernel(leaves, place, halo_c, own_c, rel, halo_x, halo_p, own_x, own_p, far, out, xs, pb, ab, lists, cnt, turns, accs):
    halo = halo_x.shape[2] // B
    total = leaves + 2 * halo
    for i in range(halo):
        cnt[i] = halo_c[0, 0, leaves - halo + i]
        cnt[halo + leaves + i] = halo_c[2, 0, i]
    for i in range(leaves):
        cnt[halo + i] = own_c[i]
    lane = lax.broadcasted_iota(jnp.int32, (R, B), 1)

    def fill(src_x, src_p, first, count):
        def one(i, carry):
            at = pl.ds(pl.multiple_of(i * B, B), B)
            to = pl.ds(pl.multiple_of((first + i) * B, B), B)
            x = jnp.where(lane < cnt[first + i], src_x[:, at], 0.0)
            high = x.astype(jnp.bfloat16)
            xs[0:R, to] = high
            xs[R : 2 * R, to] = (x - high.astype(jnp.float32)).astype(jnp.bfloat16)
            pb[0:3, to] = src_p[:, at] * 4.0
            return carry

        lax.fori_loop(0, count, one, 0, unroll=4)

    fill(halo_x.at[0], halo_p.at[0], 0, halo)
    fill(own_x, own_p, halo, leaves)
    fill(halo_x.at[1], halo_p.at[1], halo + leaves, halo)
    tail = pl.ds(total * B, 2 * LANES)
    xs[:, tail] = jnp.zeros((2 * R, 2 * LANES), jnp.bfloat16)
    pb[:, tail] = jnp.zeros((8, 2 * LANES), jnp.float32)

    def prepare(slot, target):
        at = slot * 24
        for n in range(NEAR):
            src = rel[target, n] - place[1]
            lists[at] = 2 * src
            lists[at + 1] = 2 * src + 1
            at = at + 1 + (cnt[src] > LANES).astype(jnp.int32)
        for n in range(3):
            lists[at + n] = 2 * total
        turns[slot] = (at - slot * 24 + 1) // 2
        for half in range(B // LANES):
            at = pl.ds(pl.multiple_of((halo + target) * B + half * LANES, LANES), LANES)
            flipped = pb[:, at].T
            for d in range(3):
                ab[slot, d, half * LANES : (half + 1) * LANES, :] = jnp.broadcast_to(
                    flipped[:, d : d + 1], (LANES, LANES)
                )

    def finish(slot, target):
        parts = []
        for half in range(B // LANES):
            rows = []
            for t in range(half * LANES // TILE, (half + 1) * LANES // TILE):
                rows.append(
                    pltpu.matmul_pop(accs[0][slot][t])[:, :LANES] + pltpu.matmul_pop(accs[1][slot][t])[:, :LANES]
                )
            flipped = jnp.concatenate(rows, axis=0).T
            parts.append(flipped[0:R] + flipped[R : 2 * R])
        at = pl.ds(pl.multiple_of(target * B, B), B)
        value = jnp.concatenate(parts, axis=1) + far[:, at]
        out[:, at] = jnp.where(lane < cnt[halo + target], value, 0.0)

    def couple_chunk(slot, tiles, units, first):
        blocks = []
        for unit in units:
            cols, weights = [], []
            for half in range(2):
                at = lists[first + 2 * unit + half]
                at = pl.ds(pl.multiple_of(at * LANES, LANES), LANES)
                weights.append(xs[:, at])
                cols.append([pb[d : d + 1, at] for d in range(3)])
            w = jnp.concatenate(weights, axis=1)
            pltpu.matmul_push_rhs(jnp.concatenate([w] * 4, axis=0), 0, unit, transpose=True)
            blocks.append(cols)
        for t in range(tiles):
            rows = pl.ds(t * TILE, TILE)
            own = [ab[slot, d, rows, :] for d in range(3)]
            for unit in units:
                highs, lows = [], []
                for half in range(2):
                    col = blocks[unit][half]
                    d0, d1, d2 = (own[d] - col[d] for d in range(3))
                    k = lax.rsqrt(((1.0 + d0 * d0) + d1 * d1) + d2 * d2)
                    high = k.astype(jnp.bfloat16)
                    highs.append(high)
                    lows.append((k - high.astype(jnp.float32)).astype(jnp.bfloat16))
                acc = accs[unit][slot][t]
                pltpu.matmul_acc_lhs(acc, jnp.concatenate(highs, axis=1), load_staged_rhs=0 if t == 0 else None)
                pltpu.matmul_acc_lhs(acc, jnp.concatenate(lows, axis=1))

    def sweep(slot, tiles):
        count = turns[slot]

        def pair(i, carry):
            couple_chunk(slot, tiles, (0, 1), slot * 24 + 4 * i)
            return carry

        lax.fori_loop(0, count // 2, pair, 0)

        @pl.when(count % 2 == 1)
        def _():
            couple_chunk(slot, tiles, (0,), slot * 24 + 2 * (count - 1))

    def group(g, carry):
        for slot in range(SLOTS):
            finish(slot, jnp.maximum(g - 1, 0) * SLOTS + slot)
            prepare(slot, jnp.minimum(g, leaves // SLOTS - 1) * SLOTS + slot)

        @pl.when(g < leaves // SLOTS)
        def _():
            for slot in range(SLOTS):
                kind = (cnt[halo + g * SLOTS + slot] + TILE - 1) // TILE - 2
                lax.switch(kind, [functools.partial(sweep, slot, tiles) for tiles in range(2, B // TILE + 1)])

        return carry

    lax.fori_loop(0, leaves // SLOTS + 1, group, 0)


def near_body(leaves, *refs):
    tiles = B // TILE
    specs = tuple(
        tuple(tuple(pltpu.ACC(unit)((TILE, 256), jnp.float32) for _ in range(tiles)) for _ in range(SLOTS))
        for unit in range(2)
    )
    pl.run_scoped(lambda accs: near_kernel(leaves, *refs, accs), specs)


def near_field(place, halo_c, own_c, rel, halo_x, halo_p, own_x, own_p, far):
    leaves = own_x.shape[1] // B
    extent = leaves + 2 * (halo_x.shape[2] // B)
    wide = extent * B + 2 * LANES
    vmem = pl.BlockSpec(memory_space=pltpu.VMEM)
    smem = pl.BlockSpec(memory_space=pltpu.SMEM)
    return pl.pallas_call(
        functools.partial(near_body, leaves),
        out_shape=jax.ShapeDtypeStruct((R, leaves * B), jnp.float32),
        in_specs=[smem] * 4 + [vmem] * 5,
        out_specs=vmem,
        scratch_shapes=[
            pltpu.VMEM((2 * R, wide), jnp.bfloat16),
            pltpu.VMEM((8, wide), jnp.float32),
            pltpu.VMEM((SLOTS, 3, B, LANES), jnp.float32),
            pltpu.SMEM((SLOTS * 24,), jnp.int32),
            pltpu.SMEM((extent,), jnp.int32),
            pltpu.SMEM((SLOTS,), jnp.int32),
        ],
        compiler_params=pltpu.CompilerParams(vmem_limit_bytes=NEAR_VMEM),
        cost_estimate=pl.CostEstimate(flops=10**9, bytes_accessed=10**7, transcendentals=10**7),
        name="near_field",
    )(place, halo_c, own_c, rel, halo_x, halo_p, own_x, own_p, far)


MESH = pl.DeviceIdType.MESH
HALF = 64
PIECES = 4
FAR_VMEM = 48 * 1024 * 1024
NT = (((1,), (1,)), ((), ()))
NN = (((1,), (0,)), ((), ()))


def split(x):
    high = x.astype(jnp.bfloat16)
    return high, (x - high.astype(jnp.float32)).astype(jnp.bfloat16)


def dot(a, b, dims):
    return lax.dot_general(a, b, dims, preferred_element_type=jnp.float32)


def dot_split(a, b, dims):
    a_high, a_low = split(a)
    b_high, b_low = split(b)
    rows = a.shape[0]
    both = dot(jnp.concatenate([a_high, a_low], axis=0), b_high, dims)
    return both[:rows] + both[rows:] + dot(a_high, b_low, dims)


def swap(x):
    return pltpu.roll(x, HALF, 1)


def fold(x):
    lane = lax.broadcasted_iota(jnp.int32, (16, LANES), 1)
    return jnp.where(lane < HALF, x[:16], x[16:])


def far_kernel(
    shape,
    count_smem, parent, box_parent, far1, far2,
    points, rhs, basis, transfer, nodes, box_transfer, nodes2, counts,
    halo_x, halo_p, halo_c, g_out,
    x_v, basis_v, transfer_v, m1, acc, part, partial, m2, own_n, own_n2, all_n2,
    load_sems, halo_send, halo_recv, x_send, x_recv, y_send, y_recv, r_send, r_recv, d_send, d_recv, z_send, z_recv,
):
    n_grp, n_dev, n_x = shape
    grp, dev = lax.axis_index("grp"), lax.axis_index("dev")
    n_y = n_dev // n_x
    my_y, my_x = dev // n_x, lax.rem(dev, n_x)
    leaves = parent.shape[0]
    boxes = box_parent.shape[0]
    reach = halo_x.shape[2]
    units = boxes + boxes // 4
    lane = lax.broadcasted_iota(jnp.int32, (R, LANES), 1)
    low = lane < HALF

    loads = [
        pltpu.make_async_copy(rhs, x_v, load_sems.at[0]),
        pltpu.make_async_copy(basis, basis_v, load_sems.at[1]),
        pltpu.make_async_copy(transfer, transfer_v, load_sems.at[2]),
    ]
    for copy in loads:
        copy.start()

    barrier = pltpu.get_barrier_semaphore()
    for step in range(1, n_dev):
        pl.semaphore_signal(barrier, inc=1, device_id={"dev": lax.rem(dev + step, n_dev)}, device_id_type=MESH)
    for step in range(1, n_grp):
        pl.semaphore_signal(barrier, inc=1, device_id={"grp": lax.rem(grp + step, n_grp)}, device_id_type=MESH)
    pl.semaphore_wait(barrier, n_dev - 1 + n_grp - 1)

    def remote(src, dst, send, recv, **place):
        return pltpu.make_async_remote_copy(
            src_ref=src, dst_ref=dst, send_sem=send, recv_sem=recv, device_id=place, device_id_type=MESH
        )

    width = x_v.shape[1]
    part_w = reach // PIECES
    halo = []
    for side in range(2):
        to = lax.rem(dev + (1 if side == 0 else n_dev - 1), n_dev)
        first = width - reach if side == 0 else 0
        for piece in range(PIECES):
            halo.append(
                remote(
                    rhs.at[:, pl.ds(first + piece * part_w, part_w)],
                    halo_x.at[side, :, pl.ds(piece * part_w, part_w)],
                    halo_send.at[side, piece],
                    halo_recv.at[side, piece],
                    dev=to,
                )
            )
        halo.append(
            remote(points.at[:, pl.ds(first, reach)], halo_p.at[side], halo_send.at[side, PIECES], halo_recv.at[side, PIECES], dev=to)
        )
        halo.append(
            remote(counts.at[0], halo_c.at[2 * side], halo_send.at[side, PIECES + 1], halo_recv.at[side, PIECES + 1], dev=to)
        )
    per = PIECES + 2

    def start_halo(which):
        for side in range(2):
            for i in which:
                halo[side * per + i].start()

    start_halo([PIECES, PIECES + 1, 0])

    acc[...] = jnp.zeros_like(acc)
    loads[0].wait()
    loads[1].wait()
    loads[2].wait()
    slot = lax.broadcasted_iota(jnp.int32, (R, B), 1)

    def lift(p, carry):
        expansions = []
        for i in range(2):
            c = 2 * p + i
            at = pl.ds(pl.multiple_of(c * B, B), B)
            x = jnp.where(slot < count_smem[c], x_v[:, at], 0.0)
            x_high, x_low = split(x)
            b_high, b_low = split(basis_v[:, at])
            both = dot(jnp.concatenate([x_high, x_low], axis=0), jnp.concatenate([b_high, b_low], axis=0), NT)
            top, bottom = both[:R], both[R:]
            expansions.append((top + bottom + swap(top))[:, :HALF])
        slab = transfer_v[:, pl.ds(pl.multiple_of(p * LANES, LANES), LANES)]
        out = dot_split(jnp.concatenate(expansions, axis=0), slab, NN)
        value = jnp.where(low, out[:R], out[R:])
        owner = jnp.where(low, parent[2 * p], parent[2 * p + 1]) - (grp * n_dev + dev) * boxes
        for b in range(boxes):
            acc[b] += jnp.where(owner == b, value, 0.0)
        return carry

    lax.fori_loop(0, leaves // 2, lift, 0, unroll=2)

    for b in range(boxes):
        full = acc[b] + swap(acc[b])
        acc[b] = full
        m1[dev * units + b] = fold(full)
    for q in range(boxes // 2):
        row = q % 2 * 8
        m1[dev * units + boxes + q // 2, row : row + 3, :] = nodes[:, q * LANES : (q + 1) * LANES]
    own_block = m1.at[pl.ds(dev * units, units)]
    x_copies = []
    for step in range(1, n_x):
        to = my_y * n_x + lax.rem(my_x + step, n_x)
        copy = remote(own_block, own_block, x_send.at[step - 1], x_recv.at[step - 1], dev=to)
        copy.start()
        x_copies.append(copy)

    sums = [jnp.zeros((16, LANES), jnp.float32) for _ in range(n_dev)]
    for q in range(boxes // 2):
        pair = jnp.concatenate([acc[2 * q], acc[2 * q + 1]], axis=0)[:, :HALF]
        out = dot_split(pair, box_transfer[:, q * LANES : (q + 1) * LANES], NN)
        for i in range(2):
            half = jnp.where(low == (i == 0), out[i * R : (i + 1) * R], 0.0)
            folded = fold(half + swap(half))
            owner = box_parent[2 * q + i] - grp * n_dev
            for p in range(n_dev):
                sums[p] += jnp.where(owner == p, folded, 0.0)
    for p in range(n_dev):
        partial[p] = sums[p]
    r_copies = []
    for step in range(1, n_dev):
        to = lax.rem(dev + step, n_dev)
        copy = remote(partial.at[to], part.at[step - 1], r_send.at[step - 1], r_recv.at[step - 1], dev=to)
        copy.start()
        r_copies.append(copy)
    start_halo([1])

    for q in range(boxes // 2):
        own_n[q * LANES : (q + 1) * LANES, :] = (
            jnp.concatenate([nodes[:, q * LANES : (q + 1) * LANES], jnp.zeros((5, LANES), jnp.float32)], axis=0) * 4.0
        ).T
    for q in range(n_dev // 2):
        at = pl.ds(pl.multiple_of((grp * n_dev // 2 + q) * LANES, LANES), LANES)
        flipped = (jnp.concatenate([nodes2[:, at], jnp.zeros((5, LANES), jnp.float32)], axis=0) * 4.0).T
        own_n2[2 * q] = flipped[:K]
        own_n2[2 * q + 1] = flipped[K:]

    def spread_nodes(q, carry):
        all_n2[q, 0:3, :] = nodes2[:, pl.ds(pl.multiple_of(q * LANES, LANES), LANES)]
        return carry

    lax.fori_loop(0, nodes2.shape[1] // LANES, spread_nodes, 0, unroll=8)

    total = partial[dev]
    for step in range(1, n_dev):
        r_copies[step - 1].wait_recv()
        total += part[step - 1]
    m2[grp, dev] = total
    d_copies = []
    for step in range(1, n_dev):
        to = lax.rem(dev + step, n_dev)
        copy = remote(m2.at[grp, dev], m2.at[grp, dev], d_send.at[step - 1], d_recv.at[step - 1], dev=to)
        copy.start()
        d_copies.append(copy)
    for copy in x_copies:
        copy.wait_recv()
    y_copies = []
    for step in range(1, n_y):
        to = lax.rem(my_y + step, n_y) * n_x + my_x
        row_block = m1.at[pl.ds(my_y * n_x * units, n_x * units)]
        copy = remote(row_block, row_block, y_send.at[step - 1], y_recv.at[step - 1], dev=to)
        copy.start()
        y_copies.append(copy)
    start_halo(range(2, PIECES))
    for copy in d_copies:
        copy.wait_recv()
    z_copies = []
    for step in range(1, n_grp):
        to = lax.rem(grp + step, n_grp)
        copy = remote(m2.at[grp], m2.at[grp], z_send.at[step - 1], z_recv.at[step - 1], grp=to)
        copy.start()
        z_copies.append(copy)

    def couple(own, sources):
        spread = [jnp.broadcast_to(own[:, d : d + 1], (K, LANES)) for d in range(3)]
        total = jnp.zeros((R, K), jnp.float32)
        for first in range(0, len(sources), 4):
            highs, lows, parts = [], [], []
            for i in range(first, first + 4, 2):
                (v0, n0, odd0), (v1, n1, odd1) = sources[i], sources[i + 1]
                value = jnp.where(
                    low, jnp.concatenate([v0, swap(v0)], axis=0), jnp.concatenate([swap(v1), v1], axis=0)
                )
                n0 = jnp.where(odd0, swap(n0), n0)
                n1 = jnp.where(odd1, n1, swap(n1))
                place = jnp.where(low[:3], n0, n1) * 4.0
                d0, d1, d2 = (spread[d] - place[d : d + 1] for d in range(3))
                high, rest = split(lax.rsqrt(((1.0 + d0 * d0) + d1 * d1) + d2 * d2))
                highs.append(high)
                lows.append(rest)
                parts.append(value)
            value = jnp.concatenate(parts, axis=1)
            value_high, value_low = split(value)
            high, rest = jnp.concatenate(highs, axis=1), jnp.concatenate(lows, axis=1)
            both = dot(jnp.concatenate([value_high, value_low], axis=0), high, NT)
            total += both[:R] + both[R:] + dot(value_high, rest, NT)
        return total

    for copy in y_copies:
        copy.wait_recv()

    def level_one(t, carry):
        sources = []
        for i in range(far1.shape[1]):
            s = lax.rem(far1[t, i], n_dev * boxes)
            home, box = lax.div(s, boxes), lax.rem(s, boxes)
            v = m1[home * units + box]
            both = m1[home * units + boxes + lax.div(box, 4)]
            n = jnp.where(lax.rem(lax.div(box, 2), 2) == 1, both[8:11], both[0:3])
            sources.append((v, n, lax.rem(box, 2) == 1))
        own = own_n[pl.ds(pl.multiple_of(t * K, K), K), :]
        acc[t, :, 0:HALF] = couple(own, sources)
        return carry

    lax.fori_loop(0, boxes, level_one, 0)

    for copy in z_copies:
        copy.wait_recv()

    def level_two(t, carry):
        target = box_parent[t]
        sources = []
        for i in range(far2.shape[1]):
            s = far2[target, i]
            v = m2[lax.div(s, n_dev), lax.rem(s, n_dev)]
            n = all_n2[lax.div(s, 2)][:3]
            sources.append((v, n, lax.rem(s, 2) == 1))
        own = own_n2[lax.rem(target, n_dev)]
        acc[t, :, HALF:LANES] = couple(own, sources)
        return carry

    lax.fori_loop(0, boxes, level_two, 0)

    for q in range(boxes // 2):
        rows = []
        for i in range(2):
            coarse = acc[2 * q + i]
            rows.append(jnp.where(low, swap(coarse), 0.0) if i == 0 else jnp.where(low, 0.0, coarse))
        moved = dot_split(jnp.concatenate(rows, axis=0), box_transfer[:, q * LANES : (q + 1) * LANES], NT)
        for i in range(2):
            g = acc[2 * q + i][:, :HALF] + moved[i * R : (i + 1) * R]
            g_out[2 * q + i] = jnp.concatenate([g, g], axis=1)

    for copies in (x_copies, r_copies, d_copies, y_copies, z_copies):
        for copy in copies:
            copy.wait_send()
    for copy in halo:
        copy.wait()


def far_field(mesh_shape, count, parent, box_parent, far1, far2, points, rhs, basis, transfer, nodes, box_transfer, nodes2):
    n_grp, n_dev, n_x = mesh_shape
    boxes = box_parent.shape[0]
    reach = REACH * B
    width = rhs.shape[1]
    vmem = pl.BlockSpec(memory_space=pltpu.VMEM)
    smem = pl.BlockSpec(memory_space=pltpu.SMEM)
    hbm = pl.BlockSpec(memory_space=pl.ANY)
    dma = pltpu.SemaphoreType.DMA
    units = boxes + boxes // 4
    return pl.pallas_call(
        functools.partial(far_kernel, mesh_shape),
        out_shape=(
            jax.ShapeDtypeStruct((2, R, reach), jnp.float32),
            jax.ShapeDtypeStruct((2, 3, reach), jnp.float32),
            jax.ShapeDtypeStruct((3, 1, count.shape[0]), jnp.int32),
            jax.ShapeDtypeStruct((boxes, R, LANES), jnp.float32),
        ),
        in_specs=[smem] * 5 + [hbm, hbm, hbm, hbm, vmem, vmem, vmem, vmem],
        out_specs=(hbm, hbm, vmem, vmem),
        scratch_shapes=[
            pltpu.VMEM((R, width), jnp.float32),
            pltpu.VMEM((K, width), jnp.float32),
            pltpu.VMEM(transfer.shape, jnp.float32),
            pltpu.VMEM((n_dev * units, 16, LANES), jnp.float32),
            pltpu.VMEM((boxes, R, LANES), jnp.float32),
            pltpu.VMEM((n_dev - 1, 16, LANES), jnp.float32),
            pltpu.VMEM((n_dev, 16, LANES), jnp.float32),
            pltpu.VMEM((n_grp, n_dev, 16, LANES), jnp.float32),
            pltpu.VMEM((boxes * K, 8), jnp.float32),
            pltpu.VMEM((n_dev, K, 8), jnp.float32),
            pltpu.VMEM((nodes2.shape[1] // LANES, 8, LANES), jnp.float32),
            dma((3,)),
            dma((2, PIECES + 2)), dma((2, PIECES + 2)),
            dma((n_x - 1,)), dma((n_x - 1,)),
            dma((n_dev // n_x - 1,)), dma((n_dev // n_x - 1,)),
            dma((n_dev - 1,)), dma((n_dev - 1,)),
            dma((n_dev - 1,)), dma((n_dev - 1,)),
            dma((n_grp - 1,)), dma((n_grp - 1,)),
        ],
        compiler_params=pltpu.CompilerParams(collective_id=0, has_side_effects=True, vmem_limit_bytes=FAR_VMEM),
        cost_estimate=pl.CostEstimate(flops=10**9, bytes_accessed=10**7, transcendentals=10**6),
        name="far_field",
    )(count, parent, box_parent, far1, far2, points, rhs, basis, transfer, nodes, box_transfer, nodes2, count.reshape(1, 1, -1))


def down_kernel(parent, first_box, g, transfer, basis, out):
    low = lax.broadcasted_iota(jnp.int32, (R, LANES), 1) < HALF

    def one(p, carry):
        top = g[parent[2 * p] - first_box[0]]
        bottom = g[parent[2 * p + 1] - first_box[0]]
        rows = jnp.concatenate([jnp.where(low, top, 0.0), jnp.where(low, 0.0, bottom)], axis=0)
        slab = transfer[:, pl.ds(pl.multiple_of(p * LANES, LANES), LANES)]
        moved = dot_split(rows, slab, NT)
        high, rest = split(moved)
        left = jnp.concatenate([high, rest, high], axis=1)
        for i in range(2):
            at = pl.ds(pl.multiple_of((2 * p + i) * B, B), B)
            b_high, b_low = split(basis[:, at])
            out[:, at] = dot(left[i * R : (i + 1) * R], jnp.concatenate([b_high, b_high, b_low], axis=0), NN)
        return carry

    lax.fori_loop(0, parent.shape[0] // 2, one, 0, unroll=2)


def down(parent, first_box, g, transfer, basis):
    vmem = pl.BlockSpec(memory_space=pltpu.VMEM)
    smem = pl.BlockSpec(memory_space=pltpu.SMEM)
    return pl.pallas_call(
        down_kernel,
        out_shape=jax.ShapeDtypeStruct((R, basis.shape[1]), jnp.float32),
        in_specs=[smem, smem, vmem, vmem, vmem],
        out_specs=vmem,
        compiler_params=pltpu.CompilerParams(vmem_limit_bytes=FAR_VMEM),
        cost_estimate=pl.CostEstimate(flops=10**8, bytes_accessed=10**7, transcendentals=0),
        name="down",
    )(parent, first_box, g, transfer, basis)


def local(
    mesh_shape,
    points,
    rhs,
    leaf_count,
    near_list,
    leaf_basis,
    leaf_transfer,
    leaf_parent,
    nodes1,
    box_transfer,
    box_parent,
    far1,
    nodes2,
    far2,
):
    leaves = leaf_count.shape[0]
    boxes = box_parent.shape[0]
    device = lax.axis_index("grp") * lax.axis_size("dev") + lax.axis_index("dev")
    halo_x, halo_p, halo_c, g = far_field(
        mesh_shape, leaf_count, leaf_parent, box_parent, far1, far2,
        points, rhs, leaf_basis, leaf_transfer, nodes1, box_transfer, nodes2,
    )
    place = jnp.stack([device * boxes, device * leaves - REACH])
    far = down(leaf_parent, place, g, leaf_transfer, leaf_basis)
    return near_field(place, halo_c, leaf_count, near_list, halo_x, halo_p, rhs, points, far)


def solution(mesh):
    placed = (
        P(None, ("grp", "dev")),
        P(None, ("grp", "dev")),
        P(("grp", "dev")),
        P(("grp", "dev"), None),
        P(None, ("grp", "dev")),
        P(None, ("grp", "dev")),
        P(("grp", "dev")),
        P(None, ("grp", "dev")),
        P(None, ("grp", "dev")),
        P(("grp", "dev")),
        P(("grp", "dev"), None),
        P(),
        P(),
    )
    mesh_shape = (mesh.shape["grp"], mesh.shape["dev"], 4)
    return jax.shard_map(
        functools.partial(local, mesh_shape),
        mesh=mesh, in_specs=placed, out_specs=P(None, ("grp", "dev")), check_vma=False
    )
```

time: 269 us -> 166 us (0.62); the launches traced: 265 us -> 166 us
  Pallas kernels: 77.6 us -> 153 us
  waiting for transfers between devices: 45.7 us -> 0 us
  matrix products: 35.4 us -> 0 us
  starting transfers between devices: 33.6 us -> 0 us
  other arithmetic: 25.7 us -> 0.07 us
  local copies, waits for them, and re-layouts: 33 us -> 13.4 us
  between operations: 14.3 us -> 0.05 us
    pallas_call x0 -> x2, Pallas kernels: none -> 77.6 us  [the longest x1 69 us: far_field(): pl.pallas_call(functools.partial(far_kernel, mesh_shape), out_shape=(jax....]
    all_gather x1 -> x0, waiting for transfers between devices: 45.7 us -> none  [gathered_total(): parts = lax.all_gather(x, axis)]
    dot_general x12 -> x0, matrix products: 35.4 us -> none  [the longest x2 13.9 us: couple(): return jnp.einsum('sij,sjr->ir', tiles, expansions, precision=HIGH)]
    all_to_all x3 -> x0, starting transfers between devices: 21.9 us -> none  [copy_for_each(): lax.all_to_all(jnp.broadcast_to(x[None], (devices, *x.shape)), axis, 0, 0...]
    all_to_all x2 -> x0, other arithmetic: 18.4 us -> none  [copy_for_each(): lax.all_to_all(jnp.broadcast_to(x[None], (devices, *x.shape)), axis, 0, 0...]
    ppermute x4 -> x0, starting transfers between devices: 11.7 us -> none  [the longest x2 8.91 us: edges(): lax.ppermute(tail, axis, [(i, i + 1) for i in range(count - 1)])]
    slice x7 -> x0, local copies, waits for them, and re-layouts: 10.3 us -> none  [the longest x1 2.46 us: local(): left[3:]]
    unnamed x74 -> x32, local copies, waits for them, and re-layouts: 6.81 us -> 13.4 us
  transfers between devices with their start and end apart: 8 -> 0, of which waited for: 1 -> 0; matrix products, arithmetic and copies ran while one was open for 17% -> 0% of each run, Pallas kernels for 0% -> 0%
where the time goes in v1:
time: 166 us
  Pallas kernels  153 us (92%)
  local copies, waits for them, and re-layouts  13.4 us (8%)
    pallas_call x1, Pallas kernels, near_field(): pl.pallas_call(functools.partial(near_body, leaves), out_shape=jax.ShapeD...  75.1 us
    pallas_call x1, Pallas kernels, far_field(): pl.pallas_call(functools.partial(far_kernel, mesh_shape), out_shape=(jax....  69 us
    unnamed x32, local copies, waits for them, and re-layouts  13.4 us
    pallas_call x1, Pallas kernels, down(): pl.pallas_call(down_kernel, out_shape=jax.ShapeDtypeStruct((R, basis.shap...  8.64 us

profile of v1, /device:TPU:1, one launch (start us, length us, event | category | flops | bytes accessed | tf_op | source)
XLA Modules:
  0.0 166.2 jit_solution(4017792483195435691)
XLA Ops:
  0.0 0.1 pad_add_fusion.first_box.refs_0_
  0.1 0.0 copy-start.11
  0.1 1.4 copy.15.refs_3_
  1.4 0.8 copy.14.far2
  2.2 0.0 copy-start
  2.2 1.2 copy-done
  3.5 0.0 copy-start.3
  3.5 0.9 copy-done.3
  4.4 0.0 copy-start.4
  4.4 0.9 copy-done.4
  5.3 0.0 copy-start.5
  5.3 0.9 copy-done.5
  6.2 0.0 copy-start.6
  6.2 0.7 copy-done.6
  6.9 0.0 copy-start.7
  6.9 0.7 copy-done.7
  7.6 0.0 copy-start.8
  7.6 0.7 copy-done.8
  8.3 0.0 copy-start.9
  8.3 0.7 copy-done.9
  8.9 0.0 copy-start.10
  8.9 0.7 copy-done.10
  9.6 0.0 copy-start.1
  9.6 69.0 %far_field.1 = (f32[2,32,8192]{2,1,0:T(8,128)S(1)}, f32[2,3,8192]{2,1,0:T(4,128)S(1)}, s32[3,1,64]{2,1,0:T(1,128)S(1)}, f32[8,32,128]{2,1,0:T(8,128)S(1)}) custom-call(s32[64]{0:T(128)S(1)} %copy-done.9, s32[64]{0:T(128)S(1)} %copy-done.8, s32[8]{0:T(128)S(1)} %copy-done.10, s32[8,16]{1,0:T(8,128)S(1)} %copy-done.7, s32[128,8]{1,0:T(8,128)S(1)} %copy.14.far2, ...), custom_call_target="tpu_custom_call" | custom-call | flops 1000000000 | bytes 10000000 | tf_op jit(solution)/shard_map/far_field/pallas_call | solution.py:473
  78.5 0.0 copy-start.12
  78.6 1.3 copy-done.12
  79.9 0.0 copy-start.13
  79.9 0.7 copy-done.13
  80.6 0.0 copy-start.14
  80.6 0.6 copy-done.14
  81.1 0.0 copy-done.11
  81.2 0.0 copy-done.1
  81.2 8.6 %down.1.refs_8_ = f32[32,16384]{1,0:T(8,128)S(1)} custom-call(s32[64]{0:T(128)S(1)} %copy-done.8, s32[2]{0:T(128)S(1)} %pad_add_fusion.first_box.refs_0_, f32[8,32,128]{2,1,0:T(8,128)S(1)} %get-tuple-element.12.g, f32[64,4096]{1,0:T(8,128)S(1)} %copy-done.1, f32[64,16384]{1,0:T(8,128)} %basis.3), custom_call_target="tpu_custom_call" | custom-call | flops 100000000 | bytes 10000000 | tf_op jit(solution)/shard_map/down/pallas_call | solution.py:532
  89.8 0.0 copy-start.2
  89.8 1.3 copy-done.2
  91.1 75.1 %near_field.1 = f32[32,16384]{1,0:T(8,128)} custom-call(s32[2]{0:T(128)} %copy-done.11, s32[3,1,64]{2,1,0:T(1,128)} %copy-done.14, s32[64]{0:T(128)} %refs_2_.1, s32[64,8]{1,0:T(8,128)} %copy.15.refs_3_, f32[2,32,8192]{2,1,0:T(8,128)} %copy-done.12, f32[2,3,8192]{2,1,0:T(4,128)} %copy-done.13, f32[32,16384]{1,0:T(8,128)} %refs_6_.1, f32[3,16384]{1,0:T(4,128)} %refs_7_.1, ...), custom_call_target="tpu_custom_call" | custom-call | flops 1000000000 | bytes 10000000 | tf_op jit(solution)/shard_map/near_field/pallas_call | solution.py:155
Async XLA Ops:
  0.1 81.1 %copy-start.11 = (s32[2]{0:T(128)}, s32[2]{0:T(128)S(1)}, u32[]{:S(2)}) copy-start(s32[2]{0:T(128)S(1)} %pad_add_fusion.first_box.refs_0_) | copy-start | bytes 28
  2.2 1.2 copy-start
  3.5 0.9 copy-start.3
  4.4 0.9 copy-start.4
  5.3 0.9 copy-start.5
  6.2 0.7 copy-start.6
  6.9 0.7 copy-start.7
  7.6 0.7 copy-start.8
  8.3 0.7 copy-start.9
  8.9 0.7 copy-start.10
  9.6 71.6 %copy-start.1 = (f32[64,4096]{1,0:T(8,128)S(1)}, f32[64,4096]{1,0:T(8,128)}, u32[]{:S(2)}) copy-start(f32[64,4096]{1,0:T(8,128)} %transfer.3) | copy-start | bytes 3145732
  78.5 1.3 copy-start.12
  79.9 0.7 copy-start.13
  80.6 0.6 copy-start.14
  89.8 1.3 copy-start.2

commit v2 on v1

v2 whole, which is shorter than its diff:
```python
import functools

import jax
import jax.numpy as jnp
from jax import lax
from jax.experimental import pallas as pl
from jax.experimental.pallas import tpu as pltpu
from jax.sharding import PartitionSpec as P

B = 256
K = 64
R = 32
NEAR = 8
REACH = 32
LANES = 128
TILE = 32
SLOTS = 2
NEAR_VMEM = 56 * 1024 * 1024


def near_kernel(leaves, place, halo_c, own_c, rel, halo_x, halo_p, own_x, own_p, far, out, xs, pb, ab, sums, lists, cnt, bases, turns, accs):
    halo = halo_x.shape[2] // B
    total = leaves + 2 * halo
    for i in range(halo):
        cnt[i] = halo_c[0, 0, leaves - halo + i]
        cnt[halo + leaves + i] = halo_c[2, 0, i]
    for i in range(leaves):
        cnt[halo + i] = own_c[i]
    lane = lax.broadcasted_iota(jnp.int32, (R, B), 1)

    def load_source(src_x, src_p, first, i):
        at = pl.ds(pl.multiple_of(i * B, B), B)
        to = pl.ds(pl.multiple_of((first + i) * B, B), B)
        x = jnp.where(lane < cnt[first + i], src_x[:, at], 0.0)
        high = x.astype(jnp.bfloat16)
        xs[0:R, to] = high
        xs[R : 2 * R, to] = (x - high.astype(jnp.float32)).astype(jnp.bfloat16)
        scaled = src_p[:, at] * 4.0
        pb[0:3, to] = scaled
        return scaled

    def load_halo(i, carry):
        load_source(halo_x.at[0], halo_p.at[0], 0, i)
        load_source(halo_x.at[1], halo_p.at[1], halo + leaves, i)
        return carry

    lax.fori_loop(0, halo, load_halo, 0, unroll=2)
    tail = pl.ds(total * B, 2 * LANES)
    xs[:, tail] = jnp.zeros((2 * R, 2 * LANES), jnp.bfloat16)
    pb[:, tail] = jnp.zeros((8, 2 * LANES), jnp.float32)

    def load_own(i, start):
        scaled = load_source(own_x, own_p, halo, i)
        padded = jnp.concatenate([scaled, jnp.zeros((5, B), jnp.float32)], axis=0)
        for half in range(B // LANES):
            flipped = padded[:, half * LANES : (half + 1) * LANES].T
            for d in range(3):
                ab[i, d, half * LANES : (half + 1) * LANES, :] = jnp.broadcast_to(
                    flipped[:, d : d + 1], (LANES, LANES)
                )
        at = start
        for n in range(NEAR):
            src = rel[n, i] - place[1]
            lists[at] = 2 * src
            lists[at + 1] = 2 * src + 1
            at = at + 1 + (cnt[src] > LANES).astype(jnp.int32)
        lists[at] = 2 * total
        chunks = (at - start + 1) // 2
        at = start + 2 * chunks
        lists[at] = lists[at - 2]
        lists[at + 1] = lists[at - 1]
        bases[i] = start
        turns[i] = chunks
        return start + 4 * ((chunks + 1) // 2)

    end = lax.fori_loop(0, leaves, load_own, 0, unroll=2)
    for i in range(4):
        lists[end + i] = 2 * total

    def push(start):
        for unit in range(2):
            parts = []
            for half in range(2):
                at = lists[start + 2 * unit + half]
                parts.append(xs[:, pl.ds(pl.multiple_of(at * LANES, LANES), LANES)])
            w = jnp.concatenate(parts, axis=1)
            pltpu.matmul_push_rhs(jnp.concatenate([w] * 4, axis=0), 0, unit, transpose=True)

    def pop(slot, target):
        for t in range(B // TILE):
            both = pltpu.matmul_pop(accs[0][slot][t]) + pltpu.matmul_pop(accs[1][slot][t])
            sums[target, t * TILE : (t + 1) * TILE, :] = both[:, :LANES]

    def couple_step(slot, tiles, target, start, split_rows):
        cols = []
        for unit in range(1 if split_rows else 2):
            halves = []
            for half in range(2):
                at = lists[start + 2 * unit + half]
                at = pl.ds(pl.multiple_of(at * LANES, LANES), LANES)
                halves.append([pb[d : d + 1, at] for d in range(3)])
            cols.append(halves)
        fresh = [True, True]
        waiting = [[], []]
        for t in range(tiles):
            own = [ab[target, d, t * TILE : (t + 1) * TILE, :] for d in range(3)]
            for unit in [t % 2] if split_rows else range(2):
                highs, lows = [], []
                for half in range(2):
                    col = cols[0 if split_rows else unit][half]
                    d0, d1, d2 = (own[d] - col[d] for d in range(3))
                    k = lax.rsqrt(((1.0 + d0 * d0) + d1 * d1) + d2 * d2)
                    high = k.astype(jnp.bfloat16)
                    highs.append(high)
                    lows.append((k - high.astype(jnp.float32)).astype(jnp.bfloat16))
                acc = accs[unit][slot][t]
                pltpu.matmul_acc_lhs(acc, jnp.concatenate(highs, axis=1), load_staged_rhs=0 if fresh[unit] else None)
                fresh[unit] = False
                for args in waiting[unit]:
                    pltpu.matmul_acc_lhs(*args)
                waiting[unit] = [(acc, jnp.concatenate(lows, axis=1))]
            if t == (1 if split_rows else 0):
                push(start + 4)
        for unit in range(2):
            for args in waiting[unit]:
                pltpu.matmul_acc_lhs(*args)

    def sweep(slot, tiles, target):
        start, count = bases[target], turns[target]

        def pair(i, carry):
            couple_step(slot, tiles, target, start + 4 * i, False)
            return carry

        lax.fori_loop(0, lax.div(count, 2), pair, 0)

        @pl.when(lax.rem(count, 2) == 1)
        def _():
            couple_step(slot, tiles, target, start + 2 * (count - 1), True)

    for slot in range(SLOTS):
        pop(slot, leaves)
    push(0)

    def group(g, carry):
        for slot in range(SLOTS):
            target = SLOTS * g + slot
            kind = lax.div(cnt[halo + target] + (TILE - 1), TILE) - 2
            lax.switch(kind, [functools.partial(sweep, slot, tiles, target) for tiles in range(2, B // TILE + 1)])
            pop(1 - slot, jnp.where(target == 0, leaves, target - 1))
        return carry

    lax.fori_loop(0, leaves // SLOTS, group, 0)
    for unit in range(2):
        pltpu.matmul_acc_lhs(accs[unit][0][0], jnp.zeros((TILE, 2 * LANES), jnp.bfloat16), load_staged_rhs=0)
    pop(1, leaves - 1)
    pop(0, leaves)

    def finish(target, carry):
        parts = []
        for half in range(B // LANES):
            flipped = sums[target, half * LANES : (half + 1) * LANES, :].T
            parts.append(flipped[0:R] + flipped[R : 2 * R])
        at = pl.ds(pl.multiple_of(target * B, B), B)
        value = jnp.concatenate(parts, axis=1) + far[:, at]
        out[:, at] = jnp.where(lane < cnt[halo + target], value, 0.0)
        return carry

    lax.fori_loop(0, leaves, finish, 0, unroll=4)


def near_body(leaves, *refs):
    tiles = B // TILE
    specs = tuple(
        tuple(tuple(pltpu.ACC(unit)((TILE, 256), jnp.float32) for _ in range(tiles)) for _ in range(SLOTS))
        for unit in range(2)
    )
    pl.run_scoped(lambda accs: near_kernel(leaves, *refs, accs), specs)


def near_field(place, halo_c, own_c, rel, halo_x, halo_p, own_x, own_p, far):
    leaves = own_x.shape[1] // B
    extent = leaves + 2 * (halo_x.shape[2] // B)
    wide = extent * B + 2 * LANES
    vmem = pl.BlockSpec(memory_space=pltpu.VMEM)
    smem = pl.BlockSpec(memory_space=pltpu.SMEM)
    return pl.pallas_call(
        functools.partial(near_body, leaves),
        out_shape=jax.ShapeDtypeStruct((R, leaves * B), jnp.float32),
        in_specs=[smem] * 4 + [vmem] * 5,
        out_specs=vmem,
        scratch_shapes=[
            pltpu.VMEM((2 * R, wide), jnp.bfloat16),
            pltpu.VMEM((8, wide), jnp.float32),
            pltpu.VMEM((leaves, 3, B, LANES), jnp.float32),
            pltpu.VMEM((leaves + 1, B, LANES), jnp.float32),
            pltpu.SMEM((leaves * 16 + 24,), jnp.int32),
            pltpu.SMEM((extent,), jnp.int32),
            pltpu.SMEM((leaves,), jnp.int32),
            pltpu.SMEM((leaves,), jnp.int32),
        ],
        compiler_params=pltpu.CompilerParams(vmem_limit_bytes=NEAR_VMEM),
        cost_estimate=pl.CostEstimate(flops=10**9, bytes_accessed=10**7, transcendentals=10**7),
        name="near_field",
    )(place, halo_c, own_c, rel, halo_x, halo_p, own_x, own_p, far)


MESH = pl.DeviceIdType.MESH
HALF = 64
PIECES = 8
FIRST_PIECES = 1
HALO_FIRST = 0
ALONG_X = (True, False)
FAR_VMEM = 62 * 1024 * 1024
NT = (((1,), (1,)), ((), ()))
NN = (((1,), (0,)), ((), ()))


def split(x):
    high = x.astype(jnp.bfloat16)
    return high, (x - high.astype(jnp.float32)).astype(jnp.bfloat16)


def dot(a, b, dims):
    return lax.dot_general(a, b, dims, preferred_element_type=jnp.float32)


def dot_split(a, b, dims):
    a_high, a_low = split(a)
    b_high, b_low = split(b)
    rows = a.shape[0]
    both = dot(jnp.concatenate([a_high, a_low], axis=0), b_high, dims)
    return both[:rows] + both[rows:] + dot(a_high, b_low, dims)


def swap(x):
    return pltpu.roll(x, HALF, 1)


def fold(x):
    lane = lax.broadcasted_iota(jnp.int32, (16, LANES), 1)
    return jnp.where(lane < HALF, x[:16], x[16:])


def far_kernel(
    shape,
    count_h, parent_h, box_parent_h, far1_h, far2_h,
    points, rhs, basis, transfer, nodes_h, box_transfer_h, nodes2_h, counts,
    halo_x, halo_p, halo_c, far_out,
    count, parent, box_parent, far1, far2, nodes, box_transfer, nodes2,
    x_v, basis_v, transfer_v, m1, near_nodes, acc, g1, part, partial, m2, own_n, own_n2, all_n2, expanded, spread_g,
    load_sems, halo_send, halo_recv, n_send, n_recv, a_send, a_recv, b_send, b_recv,
    r_send, r_recv, d_send, d_recv, z_send, z_recv, c_send, c_recv,
):
    n_grp, n_dev, n_x = shape
    grp, dev = lax.axis_index("grp"), lax.axis_index("dev")
    n_y = n_dev // n_x
    my_y, my_x = dev // n_x, lax.rem(dev, n_x)
    leaves = parent.shape[0]
    boxes = box_parent.shape[0]
    reach = halo_x.shape[2]
    half_boxes = boxes // 2
    low = lax.broadcasted_iota(jnp.int32, (R, LANES), 1) < HALF

    pairs = [
        (nodes_h, nodes), (count_h, count), (parent_h, parent), (rhs, x_v), (basis, basis_v), (transfer, transfer_v),
        (box_parent_h, box_parent), (box_transfer_h, box_transfer), (far1_h, far1), (far2_h, far2), (nodes2_h, nodes2),
    ]
    loads = [pltpu.make_async_copy(src, dst, load_sems.at[i]) for i, (src, dst) in enumerate(pairs)]
    for copy in loads:
        copy.start()

    barrier = pltpu.get_barrier_semaphore()
    for step in range(1, n_dev):
        pl.semaphore_signal(barrier, inc=1, device_id={"dev": lax.rem(dev + step, n_dev)}, device_id_type=MESH)
    for to in [lax.rem(grp + 2 * step, n_grp) for step in range(1, n_grp // 2)] + [grp + 1 - 2 * lax.rem(grp, 2)]:
        pl.semaphore_signal(barrier, inc=1, device_id={"grp": to}, device_id_type=MESH)
    pl.semaphore_wait(barrier, n_dev - 1 + n_grp // 2)

    def remote(src, dst, send, recv, **place):
        return pltpu.make_async_remote_copy(
            src_ref=src, dst_ref=dst, send_sem=send, recv_sem=recv, device_id=place, device_id_type=MESH
        )

    width = x_v.shape[1]
    part_w = reach // PIECES
    halo = []
    for side in range(2):
        to = lax.rem(dev + (1 if side == 0 else n_dev - 1), n_dev)
        first = width - reach if side == 0 else 0
        for piece in range(PIECES):
            halo.append(
                remote(
                    rhs.at[:, pl.ds(first + piece * part_w, part_w)],
                    halo_x.at[side, :, pl.ds(piece * part_w, part_w)],
                    halo_send.at[side, piece],
                    halo_recv.at[side, piece],
                    dev=to,
                )
            )
        halo.append(
            remote(points.at[:, pl.ds(first, reach)], halo_p.at[side], halo_send.at[side, PIECES], halo_recv.at[side, PIECES], dev=to)
        )
        halo.append(
            remote(counts.at[0], halo_c.at[2 * side], halo_send.at[side, PIECES + 1], halo_recv.at[side, PIECES + 1], dev=to)
        )
    per = PIECES + 2
    sends = (dev < n_dev - 1, dev > 0)

    def start_halo(which):
        for side in range(2):

            @pl.when(sends[side])
            def _():
                for i in which:
                    halo[side * per + i].start()

    loads[0].wait()
    for q in range(half_boxes):
        near_nodes[dev * (half_boxes // 2) + q // 2, q % 2 * 8 : q % 2 * 8 + 3, :] = nodes[:, q * LANES : (q + 1) * LANES]
    own_nodes = near_nodes.at[pl.ds(dev * (half_boxes // 2), half_boxes // 2)]
    n_copies = []
    for step in range(1, n_dev):
        to = lax.rem(dev + step, n_dev)
        copy = remote(own_nodes, own_nodes, n_send.at[step - 1], n_recv.at[step - 1], dev=to)
        copy.start()
        n_copies.append(copy)
    start_halo([PIECES, PIECES + 1] + list(range(FIRST_PIECES)))

    acc[...] = jnp.zeros_like(acc)
    for copy in loads[1:]:
        copy.wait()
    slot = lax.broadcasted_iota(jnp.int32, (R, B), 1)

    def expand(p, carry):
        for i in range(2):
            c = 2 * p + i
            at = pl.ds(pl.multiple_of(c * B, B), B)
            x = jnp.where(slot < count[c], x_v[:, at], 0.0)
            x_high, x_low = split(x)
            b_high, b_low = split(basis_v[:, at])
            both = dot(jnp.concatenate([x_high, x_low], axis=0), jnp.concatenate([b_high, b_low], axis=0), NT)
            top, bottom = both[:R], both[R:]
            expanded[p, i * R : (i + 1) * R, :] = top + bottom + swap(top)
        return carry

    lax.fori_loop(0, leaves // 2, expand, 0, unroll=4)

    def lift(p, carry):
        slab = transfer_v[:, pl.ds(pl.multiple_of(p * LANES, LANES), LANES)]
        out = dot_split(expanded[p][:, :HALF], slab, NN)
        value = jnp.where(low, out[:R], out[R:])
        owner = jnp.where(low, parent[2 * p], parent[2 * p + 1]) - (grp * n_dev + dev) * boxes
        for b in range(boxes):
            acc[b] += jnp.where(owner == b, value, 0.0)
        return carry

    lax.fori_loop(0, leaves // 2, lift, 0, unroll=4)

    for b in range(boxes):
        full = acc[b] + swap(acc[b])
        acc[b] = full
        m1[b // half_boxes, dev * half_boxes + b % half_boxes] = fold(full)
    first, second = [], []

    def along(which, block, to, sem, copies):
        copy = remote(block, block, a_send.at[which, sem], a_recv.at[which, sem], dev=to)
        copy.start()
        copies.append(copy)

    mine = [m1.at[i, pl.ds(dev * half_boxes, half_boxes)] for i in range(2)]
    for which, along_x in enumerate(ALONG_X):
        for step in range(1, n_x if along_x else n_y):
            to = my_y * n_x + lax.rem(my_x + step, n_x) if along_x else lax.rem(my_y + step, n_y) * n_x + my_x
            along(which, mine[which], to, step - 1, first)

    sums = [jnp.zeros((16, LANES), jnp.float32) for _ in range(n_dev)]
    for q in range(boxes // 2):
        pair = jnp.concatenate([acc[2 * q], acc[2 * q + 1]], axis=0)[:, :HALF]
        out = dot_split(pair, box_transfer[:, q * LANES : (q + 1) * LANES], NN)
        for i in range(2):
            half = jnp.where(low == (i == 0), out[i * R : (i + 1) * R], 0.0)
            folded = fold(half + swap(half))
            owner = box_parent[2 * q + i] - grp * n_dev
            for p in range(n_dev):
                sums[p] += jnp.where(owner == p, folded, 0.0)
    for p in range(n_dev):
        partial[p] = sums[p]
    r_copies = []
    for step in range(1, n_dev):
        to = lax.rem(dev + step, n_dev)
        copy = remote(partial.at[to], part.at[step - 1], r_send.at[step - 1], r_recv.at[step - 1], dev=to)
        copy.start()
        r_copies.append(copy)
    start_halo(range(FIRST_PIECES, FIRST_PIECES + 1))

    for q in range(boxes // 2):
        own_n[q * LANES : (q + 1) * LANES, :] = (
            jnp.concatenate([nodes[:, q * LANES : (q + 1) * LANES], jnp.zeros((5, LANES), jnp.float32)], axis=0) * 4.0
        ).T
    for q in range(n_dev // 2):
        at = pl.ds(pl.multiple_of((grp * n_dev // 2 + q) * LANES, LANES), LANES)
        flipped = (jnp.concatenate([nodes2[:, at], jnp.zeros((5, LANES), jnp.float32)], axis=0) * 4.0).T
        own_n2[2 * q] = flipped[:K]
        own_n2[2 * q + 1] = flipped[K:]

    def spread_nodes(q, carry):
        all_n2[q, 0:3, :] = nodes2[:, pl.ds(pl.multiple_of(q * LANES, LANES), LANES)]
        return carry

    lax.fori_loop(0, nodes2.shape[1] // LANES, spread_nodes, 0, unroll=8)

    total = partial[dev]
    for step in range(1, n_dev):
        r_copies[step - 1].wait_recv()
        total += part[step - 1]
    m2[grp, dev] = total
    d_copies = []
    for step in range(1, n_dev):
        to = lax.rem(dev + step, n_dev)
        copy = remote(m2.at[grp, dev], m2.at[grp, dev], d_send.at[step - 1], d_recv.at[step - 1], dev=to)
        copy.start()
        d_copies.append(copy)
    for copy in first:
        copy.wait_recv()
    if HALO_FIRST:
        start_halo(range(FIRST_PIECES + 1, HALO_FIRST))
    for which, along_x in enumerate(ALONG_X):
        for step in range(1, n_y if along_x else n_x):
            if along_x:
                row = m1.at[which, pl.ds(my_y * n_x * half_boxes, n_x * half_boxes)]
                to = lax.rem(my_y + step, n_y) * n_x + my_x
                copy = remote(row, row, b_send.at[which, step - 1, 0], b_recv.at[which, step - 1, 0], dev=to)
                copy.start()
                second.append(copy)
            else:
                for y in range(n_y):
                    piece = m1.at[which, pl.ds((y * n_x + my_x) * half_boxes, half_boxes)]
                    to = my_y * n_x + lax.rem(my_x + step, n_x)
                    copy = remote(piece, piece, b_send.at[which, step - 1, y], b_recv.at[which, step - 1, y], dev=to)
                    copy.start()
                    second.append(copy)
    start_halo(range(max(FIRST_PIECES + 1, HALO_FIRST), PIECES))
    for copy in d_copies:
        copy.wait_recv()
    other = grp + 1 - 2 * lax.rem(grp, 2)
    z_copies, c_copies = [], []
    for step in range(1, n_grp // 2):
        to = lax.rem(grp + 2 * step, n_grp)
        copy = remote(m2.at[grp], m2.at[grp], z_send.at[step - 1], z_recv.at[step - 1], grp=to)
        copy.start()
        z_copies.append(copy)
    copy = remote(m2.at[grp], m2.at[grp], c_send.at[0], c_recv.at[0], grp=other)
    copy.start()
    c_copies.append(copy)

    def couple(own, sources):
        spread = [jnp.broadcast_to(own[:, d : d + 1], (K, LANES)) for d in range(3)]
        total = jnp.zeros((R, K), jnp.float32)
        for first in range(0, len(sources), 4):
            highs, lows, parts = [], [], []
            for i in range(first, first + 4, 2):
                (v0, n0, odd0), (v1, n1, odd1) = sources[i], sources[i + 1]
                value = jnp.where(
                    low, jnp.concatenate([v0, swap(v0)], axis=0), jnp.concatenate([swap(v1), v1], axis=0)
                )
                n0 = jnp.where(odd0, swap(n0), n0)
                n1 = jnp.where(odd1, n1, swap(n1))
                place = jnp.where(low[:3], n0, n1) * 4.0
                d0, d1, d2 = (spread[d] - place[d : d + 1] for d in range(3))
                high, rest = split(lax.rsqrt(((1.0 + d0 * d0) + d1 * d1) + d2 * d2))
                highs.append(high)
                lows.append(rest)
                parts.append(value)
            value = jnp.concatenate(parts, axis=1)
            value_high, value_low = split(value)
            high, rest = jnp.concatenate(highs, axis=1), jnp.concatenate(lows, axis=1)
            both = dot(jnp.concatenate([value_high, value_low], axis=0), high, NT)
            total += both[:R] + both[R:] + dot(value_high, rest, NT)
        return total

    for copy in n_copies + second:
        copy.wait_recv()

    for step in range(1, n_grp // 2):
        z_copies[step - 1].wait_recv()
        block = m2.at[lax.rem(grp + n_grp - 2 * step, n_grp)]
        copy = remote(block, block, c_send.at[step], c_recv.at[step], grp=other)
        copy.start()
        c_copies.append(copy)

    def level_one(t, carry):
        sources = []
        for i in range(far1.shape[1]):
            s = lax.rem(far1[t, i], n_dev * boxes)
            home, box = lax.div(s, boxes), lax.rem(s, boxes)
            v = m1[lax.div(box, half_boxes), home * half_boxes + lax.rem(box, half_boxes)]
            both = near_nodes[home * (half_boxes // 2) + lax.div(box, 4)]
            n = jnp.where(lax.rem(lax.div(box, 2), 2) == 1, both[8:11], both[0:3])
            sources.append((v, n, lax.rem(box, 2) == 1))
        own = own_n[pl.ds(pl.multiple_of(t * K, K), K), :]
        acc[t, :, 0:HALF] = couple(own, sources)
        return carry

    lax.fori_loop(0, boxes, level_one, 0, unroll=2)

    for copy in c_copies:
        copy.wait_recv()

    def level_two(t, carry):
        target = box_parent[t]
        sources = []
        for i in range(far2.shape[0]):
            s = far2[i, target]
            v = m2[lax.div(s, n_dev), lax.rem(s, n_dev)]
            n = all_n2[lax.div(s, 2)][:3]
            sources.append((v, n, lax.rem(s, 2) == 1))
        own = own_n2[lax.rem(target, n_dev)]
        acc[t, :, HALF:LANES] = couple(own, sources)
        return carry

    lax.fori_loop(0, boxes, level_two, 0, unroll=2)

    for q in range(boxes // 2):
        rows = []
        for i in range(2):
            coarse = acc[2 * q + i]
            rows.append(jnp.where(low, swap(coarse), 0.0) if i == 0 else jnp.where(low, 0.0, coarse))
        moved = dot_split(jnp.concatenate(rows, axis=0), box_transfer[:, q * LANES : (q + 1) * LANES], NT)
        for i in range(2):
            g = acc[2 * q + i][:, :HALF] + moved[i * R : (i + 1) * R]
            g1[2 * q + i] = jnp.concatenate([g, g], axis=1)

    def descend(p, carry):
        top = g1[lax.rem(parent[2 * p], boxes)]
        bottom = g1[lax.rem(parent[2 * p + 1], boxes)]
        rows = jnp.concatenate([jnp.where(low, top, 0.0), jnp.where(low, 0.0, bottom)], axis=0)
        slab = transfer_v[:, pl.ds(pl.multiple_of(p * LANES, LANES), LANES)]
        high, rest = split(dot_split(rows, slab, NT))
        spread_g[p] = jnp.concatenate([high, rest, high], axis=1)
        return carry

    lax.fori_loop(0, leaves // 2, descend, 0, unroll=4)

    def evaluate(p, carry):
        left = spread_g[p]
        for i in range(2):
            at = pl.ds(pl.multiple_of((2 * p + i) * B, B), B)
            b_high, b_low = split(basis_v[:, at])
            far_out[:, at] = dot(left[i * R : (i + 1) * R], jnp.concatenate([b_high, b_high, b_low], axis=0), NN)
        return carry

    lax.fori_loop(0, leaves // 2, evaluate, 0, unroll=4)

    for copies in (n_copies, first, r_copies, d_copies, second, z_copies, c_copies):
        for copy in copies:
            copy.wait_send()
    for side in range(2):

        @pl.when(sends[side])
        def _():
            for copy in halo[side * per : (side + 1) * per]:
                copy.wait_send()

        @pl.when(sends[1 - side])
        def _():
            for copy in halo[side * per : (side + 1) * per]:
                copy.wait_recv()


def far_field(mesh_shape, count, parent, box_parent, far1, far2, points, rhs, basis, transfer, nodes, box_transfer, nodes2):
    n_grp, n_dev, n_x = mesh_shape
    n_y = n_dev // n_x
    boxes = box_parent.shape[0]
    leaves = count.shape[0]
    reach = REACH * B
    width = rhs.shape[1]
    vmem = pl.BlockSpec(memory_space=pltpu.VMEM)
    hbm = pl.BlockSpec(memory_space=pl.ANY)
    dma = pltpu.SemaphoreType.DMA
    small = (count, parent, box_parent, far1, far2)
    large = (nodes, box_transfer, nodes2, rhs, basis, transfer)
    return pl.pallas_call(
        functools.partial(far_kernel, mesh_shape),
        out_shape=(
            jax.ShapeDtypeStruct((2, R, reach), jnp.float32),
            jax.ShapeDtypeStruct((2, 3, reach), jnp.float32),
            jax.ShapeDtypeStruct((3, 1, leaves), jnp.int32),
            jax.ShapeDtypeStruct((R, width), jnp.float32),
        ),
        in_specs=[pl.BlockSpec(memory_space=pltpu.HBM)] * 13,
        out_specs=(hbm, hbm, hbm, vmem),
        scratch_shapes=[pltpu.SMEM(a.shape, jnp.int32) for a in small]
        + [pltpu.VMEM(a.shape, jnp.float32) for a in large]
        + [
            pltpu.VMEM((2, n_dev * (boxes // 2), 16, LANES), jnp.float32),
            pltpu.VMEM((n_dev * (boxes // 4), 16, LANES), jnp.float32),
            pltpu.VMEM((boxes, R, LANES), jnp.float32),
            pltpu.VMEM((boxes, R, LANES), jnp.float32),
            pltpu.VMEM((n_dev - 1, 16, LANES), jnp.float32),
            pltpu.VMEM((n_dev, 16, LANES), jnp.float32),
            pltpu.VMEM((n_grp, n_dev, 16, LANES), jnp.float32),
            pltpu.VMEM((boxes * K, 8), jnp.float32),
            pltpu.VMEM((n_dev, K, 8), jnp.float32),
            pltpu.VMEM((nodes2.shape[1] // LANES, 8, LANES), jnp.float32),
            pltpu.VMEM((leaves // 2, 2 * R, LANES), jnp.float32),
            pltpu.VMEM((leaves // 2, 2 * R, 3 * K), jnp.bfloat16),
            dma((11,)),
            dma((2, PIECES + 2)), dma((2, PIECES + 2)),
            dma((n_dev - 1,)), dma((n_dev - 1,)),
            dma((2, max(n_x, n_y) - 1)), dma((2, max(n_x, n_y) - 1)),
            dma((2, max(n_x, n_y) - 1, n_y)), dma((2, max(n_x, n_y) - 1, n_y)),
            dma((n_dev - 1,)), dma((n_dev - 1,)),
            dma((n_dev - 1,)), dma((n_dev - 1,)),
            dma((n_grp // 2 - 1,)), dma((n_grp // 2 - 1,)),
            dma((n_grp // 2,)), dma((n_grp // 2,)),
        ],
        compiler_params=pltpu.CompilerParams(collective_id=0, has_side_effects=True, vmem_limit_bytes=FAR_VMEM),
        cost_estimate=pl.CostEstimate(flops=10**9, bytes_accessed=10**7, transcendentals=10**6),
        name="far_field",
    )(count, parent, box_parent, far1, far2, points, rhs, basis, transfer, nodes, box_transfer, nodes2, count.reshape(1, 1, -1))


def local(
    mesh_shape,
    points,
    rhs,
    leaf_count,
    near_list,
    leaf_basis,
    leaf_transfer,
    leaf_parent,
    nodes1,
    box_transfer,
    box_parent,
    far1,
    nodes2,
    far2,
):
    leaves = leaf_count.shape[0]
    boxes = box_parent.shape[0]
    device = lax.axis_index("grp") * lax.axis_size("dev") + lax.axis_index("dev")
    halo_x, halo_p, halo_c, far = far_field(
        mesh_shape, leaf_count, leaf_parent, box_parent, far1, far2.T,
        points, rhs, leaf_basis, leaf_transfer, nodes1, box_transfer, nodes2,
    )
    place = jnp.stack([device * boxes, device * leaves - REACH])
    return near_field(place, halo_c, leaf_count, near_list.T, halo_x, halo_p, rhs, points, far)


def solution(mesh):
    placed = (
        P(None, ("grp", "dev")),
        P(None, ("grp", "dev")),
        P(("grp", "dev")),
        P(("grp", "dev"), None),
        P(None, ("grp", "dev")),
        P(None, ("grp", "dev")),
        P(("grp", "dev")),
        P(None, ("grp", "dev")),
        P(None, ("grp", "dev")),
        P(("grp", "dev")),
        P(("grp", "dev"), None),
        P(),
        P(),
    )
    mesh_shape = (mesh.shape["grp"], mesh.shape["dev"], 4)
    return jax.shard_map(
        functools.partial(local, mesh_shape),
        mesh=mesh, in_specs=placed, out_specs=P(None, ("grp", "dev")), check_vma=False
    )
```

time: 166 us -> 141 us (0.85)
  the two profiles are of different devices: /device:TPU:1 before, /device:TPU:32 now
where the time goes in v2:
time: 141 us
  Pallas kernels  141 us (100%)
    pallas_call x1, Pallas kernels, near_field(): pl.pallas_call(functools.partial(near_body, leaves), out_shape=jax.ShapeD...  80 us
    pallas_call x1, Pallas kernels, far_field(): pl.pallas_call(functools.partial(far_kernel, mesh_shape), out_shape=(jax....  60.6 us

profile of v2, /device:TPU:32, one launch (start us, length us, event | category | flops | bytes accessed | tf_op | source)
XLA Modules:
  0.0 141.2 jit_solution(6961428255101052896)
XLA Ops:
  0.0 0.6 pad_add_fusion.refs_0_
  0.6 60.6 %far_field.1 = (f32[2,32,8192]{2,1,0:T(8,128)}, f32[2,3,8192]{2,1,0:T(4,128)}, s32[3,1,64]{2,1,0:T(1,128)}, f32[32,16384]{1,0:T(8,128)}) custom-call(s32[64]{0:T(128)} %refs_2_.1, s32[64]{0:T(128)} %parent_h.1, s32[8]{0:T(128)} %box_parent_h.1, s32[8,16]{1,0:T(8,128)} %far1_h.1, s32[8,128]{1,0:T(8,128)} %bitcast.5, f32[3,16384]{1,0:T(4,128)} %refs_7_.1, ...), custom_call_target="tpu_custom_call" | custom-call | flops 1000000000 | bytes 10000000 | tf_op jit(solution)/shard_map/far_field/pallas_call | solution.py:583
  61.2 80.0 %near_field.1 = f32[32,16384]{1,0:T(8,128)} custom-call(s32[2]{0:T(128)} %pad_add_fusion.refs_0_, s32[3,1,64]{2,1,0:T(1,128)} %get-tuple-element.9.refs_1_, s32[64]{0:T(128)} %refs_2_.1, s32[8,64]{1,0:T(8,128)} %bitcast.7, f32[2,32,8192]{2,1,0:T(8,128)} %get-tuple-element.10.refs_4_, f32[2,3,8192]{2,1,0:T(4,128)} %get-tuple-element.11.refs_5_, ...), custom_call_target="tpu_custom_call" | custom-call | flops 1000000000 | bytes 10000000 | tf_op jit(solution)/shard_map/near_field/pallas_call | solution.py:187
